TPU v7x, 256 devices: a 2x2x32 block of a 4x8x32 slice. The times are simulated.
256 devices in a mesh: subj: 4 (over x, y), gx: 32 (over z), gy: 2 (over core).
Axes of the slice: x: 2, y: 2, z: 32, core: 2. Of those that a mesh axis runs over, the one named last changes fastest.
The devices are a block of a 4x8x32 slice.
Arguments:
- bold: float32 [1200, 128, 64, 32], P('subj', 'gx', 'gy'), parts along dimension 0, may hold values from -70 to 70
- brain_bounds: int32 [128, 64, 8], P('gx', 'gy', 'subj'), parts along dimension 2, may hold values from 0 to 32, as said below
- seed_index: int32 [4096], P('subj'), parts along dimension 0, may hold values from 0 to 262143
Outputs:
- connectivity: bfloat16 [128, 64, 32, 4096], P('gx', 'gy', None, 'subj'), parts along dimension 3
There are 4 independent parts, one for each index of `subj`. A program takes and returns all parts, laid end to end along the dimension named above; each array names one. Nothing has to cross between parts.
Inputs may be any that keep to these rules, and one draw needn't show every extreme that they name: `brain_bounds`: in every column the first bound is at most 16 and the second at least 16. `seed_index`: voxel number (x * 64 + y) * 32 + z; seeds may repeat.
All inputs are finite; a program needn't handle non-finite values.
Results may differ from a plain program's by a relative error of at most 0.0056.
Values may be sent and summed in bfloat16 or wider, within the bound.
No kernel may reach another device: no remote copies, remote signals or barrier semaphores. Data moves between devices by JAX's collectives and lax.ppermute only.
A program may use at most 128 MiB of HBM per device.

v0:
```python
import math

import jax
import jax.numpy as jnp
from jax import lax
from jax.sharding import PartitionSpec as P

raw_taps = [math.exp(-k * k / 8.0) for k in range(-4, 5)]
kernel_taps = [t / sum(raw_taps) for t in raw_taps]


def with_halo(shard, sides, width):
    for axis, dim in sides:
        size, length = (lax.axis_size(axis), shard.shape[dim])
        up = [(i, (i + 1) % size) for i in range(size - 1)]
        down = [(j, i) for i, j in up]
        last = lax.slice_in_dim(shard, length - width, length, axis=dim)
        initial = lax.slice_in_dim(shard, 0, width, axis=dim)
        before = lax.ppermute(last, axis, up)
        after = lax.ppermute(initial, axis, down)
        shard = jnp.concatenate([before, shard, after], axis=dim)
    return shard


def smooth_axis(padded, axis, count):
    total = kernel_taps[0] * lax.slice_in_dim(padded, 0, count, axis=axis)
    for k in range(1, 9):
        total = total + kernel_taps[k] * lax.slice_in_dim(padded, k, k + count, axis=axis)
    return total


def local(bold, brain_bounds, seed_index):
    frames, cells_x, cells_y, cells_z = bold.shape
    widened = with_halo(bold, (("gx", 1),), 4)
    along_x = smooth_axis(widened, 1, cells_x)
    widened = with_halo(along_x, (("gy", 2),), 4)
    along_y = smooth_axis(widened, 2, cells_y)
    padded = jnp.pad(along_y, ((0, 0), (0, 0), (0, 0), (4, 4)))
    smoothed = smooth_axis(padded, 3, cells_z)
    mean = jnp.mean(smoothed, axis=0)
    centered = smoothed - mean
    var = jnp.mean(centered * centered, axis=0)
    zscored = (centered * lax.rsqrt(var + 1e-06)).astype(jnp.bfloat16)
    flat = zscored.reshape(frames, cells_x * cells_y * cells_z)
    start_x = lax.axis_index("gx") * cells_x
    start_y = lax.axis_index("gy") * cells_y
    column = lax.axis_size("gy") * cells_y * cells_z
    seed_x = seed_index // column
    within = seed_index % column
    seed_y = within // cells_z
    seed_z = within % cells_z
    local_x = seed_x - start_x
    local_y = seed_y - start_y
    owned = (local_x >= 0) & (local_x < cells_x) & (local_y >= 0) & (local_y < cells_y)
    position = jnp.where(owned, (local_x * cells_y + local_y) * cells_z + seed_z, 0)
    picked = (
        jnp.take(flat, position, axis=1).astype(jnp.float32) * owned.astype(jnp.float32)[None, :]
    )
    table = lax.psum(picked, ("gx", "gy")).astype(jnp.bfloat16)
    corr = lax.dot_general(
        flat, table, (((0,), (0,)), ((), ())), preferred_element_type=jnp.float32
    )
    corr = corr * (1.0 / frames)
    depth = jnp.arange(cells_z, dtype=jnp.int32)
    inside = (depth[None, None, :] >= brain_bounds[:, :, 0:1]) & (
        depth[None, None, :] < brain_bounds[:, :, 1:2]
    )
    corr = corr.reshape(cells_x, cells_y, cells_z, -1) * inside[:, :, :, None].astype(jnp.float32)
    return corr.astype(jnp.bfloat16)


def solution(mesh):
    placed = (P("subj", "gx", "gy", None), P("gx", "gy", "subj"), P("subj"))
    return jax.shard_map(
        local, mesh=mesh, in_specs=placed, out_specs=P("gx", "gy", None, "subj"), check_vma=False
    )
```

profile of v0, /device:TPU:44, one launch (start us, length us, event | category | flops | bytes accessed | tf_op | source)
XLA Modules:
  0.0 471.1 jit_solution(15500717209150153752)
XLA Ops:
  0.0 6.6 %collective-permute-start = (f32[300,4,32,32]{0,3,2,1:T(8,128)}, f32[300,4,32,32]{0,3,2,1:T(8,128)}, u32[]{:S(2)}, u32[]{:S(2)}) collective-permute-start(f32[300,4,32,32]{0,3,2,1:T(8,128)} %param.3), channel_id=1, source_target_pairs={{0,2},{2,4},{4,6},{6,8},{8,10},{10,12},{12,14},{14,16},{16,18},{18... | collective-permute-start | bytes 14745608 | tf_op jit(solution)/shard_map/ppermute | solution.py:19
  6.6 1.3 collective-permute-start.1
  8.0 0.7 compare_and_fusion
  8.7 130.5 %collective-permute-done = f32[300,4,32,32]{0,3,2,1:T(8,128)} collective-permute-done((f32[300,4,32,32]{0,3,2,1:T(8,128)}, f32[300,4,32,32]{0,3,2,1:T(8,128)}, u32[]{:S(2)}, u32[]{:S(2)}) %collective-permute-start) | collective-permute-done | bytes 4915232 | tf_op jit(solution)/shard_map/ppermute | solution.py:19
  139.2 3.3 constant_dynamic-update-slice_fusion.1
  142.5 7.6 %constant_dynamic-update-slice_fusion = (f32[300,8,32,32]{0,3,2,1:T(8,128)S(1)}, f32[300,8,32,32]{0,3,2,1:T(8,128)}) fusion(f32[300,8,32,32]{0,3,2,1:T(8,128)S(1)} %constant_dynamic-update-slice_fusion.1, f32[300,4,32,32]{0,3,2,1:T(8,128)} %param.3), kind=kLoop, calls=%fused_computation.88 | loop fusion | bytes 17498112 | tf_op jit(solution)/shard_map/concatenate | solution.py:21
  150.1 0.0 collective-permute-done.1
  150.1 6.0 %constant_dynamic-update-slice_fusion.2 = f32[300,8,32,32]{0,3,2,1:T(8,128)} fusion(f32[300,8,32,32]{0,3,2,1:T(8,128)} %get-tuple-element.13, f32[300,4,32,32]{0,3,2,1:T(8,128)} %collective-permute-done.1), kind=kLoop, calls=%fused_computation.90 | loop fusion | bytes 12582912 | tf_op jit(solution)/shard_map/concatenate | solution.py:21
  156.0 0.0 copy-start.1
  156.0 17.5 %fusion.39 = f32[300,4,32,32]{0,3,2,1:T(8,128)} fusion(f32[300,8,32,32]{0,3,2,1:T(8,128)} %constant_dynamic-update-slice_fusion.2, f32[300,8,32,32]{0,3,2,1:T(8,128)S(1)} %get-tuple-element.12, f32[300,4,32,32]{0,3,2,1:T(8,128)} %collective-permute-done.1, f32[300,4,32,32]{0,3,2,1:T(8,128)} %param.3, f32[300,4,32,32]{0,3,2,1:T(8,128)} %collective-permute-done), kind=kLoop, calls=%fused_computation.65 | loop fusion | flops 20889600 | bytes 49152000 | tf_op jit(solution)/shard_map/add | solution.py:28
  173.5 1.5 fusion.59
  175.1 1.4 collective-permute-start.2
  176.4 1.5 collective-permute-start.3
  177.9 0.0 copy-done.1
  178.0 0.1 fusion.48
  178.1 0.2 collective-permute-done.2
  178.3 2.4 collective-permute-done.3
  180.6 25.4 %fusion.3 = f32[300,4,32,32]{0,3,2,1:T(8,128)} fusion(f32[300,4,32,32]{0,3,2,1:T(8,128)} %fusion.39, f32[300,4,4,32]{0,3,2,1:T(8,128)S(1)} %collective-permute-done.3, f32[300,4,4,32]{0,3,2,1:T(8,128)S(1)} %collective-permute-done.2), kind=kLoop, calls=%fused_computation.26 | loop fusion | flops 30720000 | bytes 11059200 | tf_op jit(solution)/shard_map/add | solution.py:28
  206.0 24.0 %fusion.57 = (f32[4,32,32]{2,1,0:T(8,128)S(1)}, f32[300,4,32,32]{0,3,2,1:T(8,128)}) fusion(f32[300,4,32,32]{0,3,2,1:T(8,128)} %fusion.3), kind=kLoop, calls=%fused_computation.115 | loop fusion | flops 22114304 | bytes 9846784 | tf_op jit(solution)/shard_map/reduce_sum | solution.py:40
  230.0 0.0 copy-start
  230.0 3.8 multiply_reduce_fusion
  233.8 0.8 copy-done
  234.6 1.2 multiply_convert_fusion.1
  235.9 5.0 %gather_fusion = bf16[1024,300]{1,0:T(8,128)(2,1)} fusion(bf16[300,4096]{0,1:T(8,128)(2,1)S(1)} %bitcast.9, s32[1024]{0:T(1024)S(1)} %broadcast_clamp_fusion), kind=kCustom, calls=%fused_computation | custom fusion | bytes 1232896 | tf_op jit(solution)/shard_map/jit(_take)/gather | solution.py:57
  240.9 2.6 multiply_bitcast_fusion
  243.5 218.0 %all-reduce.2 = bf16[300,1024]{0,1:T(8,128)(2,1)} all-reduce(f32[300,1024]{0,1:T(8,128)} %multiply_bitcast_fusion), channel_id=1, replica_groups=mesh['subj'=4,'gx'=32,'gy'=2] {'gx','gy'}, use_global_device_ids=true, to_apply=%region_2.3 | all-reduce | flops 307200 | bytes 1843200 | tf_op jit(solution)/shard_map/psum | solution.py:59
  461.5 5.7 %convolution_multiply_fusion = f32[4096,1024]{1,0:T(8,128)S(1)} fusion(bf16[300,4096]{0,1:T(8,128)(2,1)S(1)} %bitcast.10, bf16[300,1024]{0,1:T(8,128)(2,1)} %all-reduce.2), kind=kOutput, calls=%fused_computation.16 | convolution fusion | flops 2520776704 | bytes 19849216 | tf_op jit(solution)/shard_map/dot_general | solution.py:60
  467.1 3.9 multiply_convert_fusion
  (5 shorter events, 0.0 us)
Async XLA Ops:
  0.0 139.2 %collective-permute-start = (f32[300,4,32,32]{0,3,2,1:T(8,128)}, f32[300,4,32,32]{0,3,2,1:T(8,128)}, u32[]{:S(2)}, u32[]{:S(2)}) collective-permute-start(f32[300,4,32,32]{0,3,2,1:T(8,128)} %param.3), channel_id=1, source_target_pairs={{0,2},{2,4},{4,6},{6,8},{8,10},{10,12},{12,14},{14,16},{16,18},{18... | collective-permute-start | bytes 14745608 | tf_op jit(solution)/shard_map/ppermute | solution.py:19
  6.6 143.4 %collective-permute-start.1 = (f32[300,4,32,32]{0,3,2,1:T(8,128)}, f32[300,4,32,32]{0,3,2,1:T(8,128)}, u32[]{:S(2)}, u32[]{:S(2)}) collective-permute-start(f32[300,4,32,32]{0,3,2,1:T(8,128)} %param.3), channel_id=1, source_target_pairs={{2,0},{4,2},{6,4},{8,6},{10,8},{12,10},{14,12},{16,14},{18,16},{20... | collective-permute-start | bytes 14745608 | tf_op jit(solution)/shard_map/ppermute | solution.py:20
  156.0 21.9 %copy-start.1 = (s32[4,32,2]{1,2,0:T(2,128)S(1)}, s32[4,32,2]{1,2,0:T(2,128)}, u32[]{:S(2)}) copy-start(s32[4,32,2]{1,2,0:T(2,128)} %param.4) | copy-start | bytes 3076
  175.1 3.2 collective-permute-start.2
  176.4 4.2 collective-permute-start.3
  230.0 4.6 copy-start
where the time goes:
time: 472 us; the launch traced here: 471 us
  blocking collectives  218 us (46%)
  waiting for transfers between devices  133 us (28%)
  other arithmetic  79.3 us (17%)
  local copies, waits for them, and re-layouts  24.2 us (5%)
  starting transfers between devices  10.8 us (2%)
  matrix products  5.67 us (1%)
    psum x1, blocking collectives, local(): table = lax.psum(picked, ('gx', 'gy')).astype(jnp.bfloat16)  218 us
    ppermute x2, waiting for transfers between devices, with_halo(): before = lax.ppermute(last, axis, up)  131 us
    add x2, other arithmetic, smooth_axis(): total + kernel_taps[k] * lax.slice_in_dim(padded, k, k + count, axis=axis)  42.9 us
    reduce_sum x1, other arithmetic, local(): mean = jnp.mean(smoothed, axis=0)  24 us
    concatenate x2, local copies, waits for them, and re-layouts, with_halo(): shard = jnp.concatenate([before, shard, after], axis=dim)  13.5 us
  transfers between devices with their start and end apart: 4, of which 3 were waited for; matrix products, arithmetic and copies ran while one was open for 2% of the time, Pallas kernels for 0%

commit v1 on v0

v1 whole, which is shorter than its diff:
```python
import functools
import math

import jax
import jax.numpy as jnp
import numpy as np
from jax import lax
from jax.experimental import pallas as pl
from jax.experimental.pallas import tpu as pltpu
from jax.sharding import PartitionSpec as P


raw_taps = [math.exp(-k * k / 8.0) for k in range(-4, 5)]
kernel_taps = [t / sum(raw_taps) for t in raw_taps]
TAP_SUM = sum(raw_taps)
REACH = 4
LANES = 128
BF = jnp.bfloat16
F32 = jnp.float32
PAIRS = (4, 8, 4)
NCHUNK = len(PAIRS)
HALF = 32
LIST = 2 * HALF
VMEM = 56 * 1024 * 1024


def dot(a, b, dims=(((1,), (0,)), ((), ()))):
    return lax.dot_general(a, b, dims, preferred_element_type=F32)


def split(a):
    high = a.astype(BF)
    return high, (a - high.astype(F32)).astype(BF)


def in_plane_kernel(side_ref, bold_ref, edge_ref, high_ref, low_ref, *refs, frames):
    chunks, rests, wide = refs[:NCHUNK], refs[NCHUNK : 2 * NCHUNK], refs[2 * NCHUNK]
    rows, cells_z = bold_ref.shape[1], bold_ref.shape[2]
    lanes = wide.shape[2]
    keep = lax.broadcasted_iota(jnp.int32, (1, 1, lanes), 2) < frames
    side = side_ref[0]
    taps_high, taps_low = high_ref[...], low_ref[...]
    group = taps_high.shape[0] // cells_z

    def along_z(block, count):
        block = jnp.where(keep, block, 0.0)
        mean = jnp.sum(block, axis=-1, keepdims=True) * (1.0 / frames)
        block = jnp.where(keep, block - mean, 0.0).reshape(count * cells_z, lanes)
        size = count * cells_z
        head, rest = split(block)
        th, tl = taps_high[:size, :size], taps_low[:size, :size]
        return (dot(th, head) + dot(th, rest) + dot(tl, head)).reshape(count, cells_z, lanes)

    for at in range(0, rows, group):
        wide[REACH + at : REACH + at + group] = along_z(bold_ref[0, at : at + group], group)
    edge = along_z(edge_ref[0], REACH)
    wide[:REACH] = jnp.where(side == 1, edge, 0.0)
    wide[REACH + rows :] = jnp.where(side == 1, 0.0, edge)

    def one_pair(index, at):
        first_row = 2 * (sum(PAIRS[:index]) + at)

        def along_y(row):
            total = kernel_taps[REACH] * wide[row + REACH]
            for k in range(1, REACH + 1):
                total = total + kernel_taps[REACH + k] * (wide[row + REACH - k] + wide[row + REACH + k])
            return total

        first, second = along_y(first_row), along_y(first_row + 1)
        last = first[:, 2 * LANES :] + pltpu.roll(second[:, 2 * LANES :], LANES // 2, 1)
        pieces = (first[:, :LANES], first[:, LANES : 2 * LANES], second[:, :LANES], second[:, LANES : 2 * LANES], last)
        for k, piece in enumerate(pieces):
            head, tail = split(piece)
            chunks[index][k, 0, at] = head
            rests[index][k, 0, at] = tail

    for index in range(NCHUNK):
        lax.fori_loop(0, PAIRS[index], lambda at, _, index=index: one_pair(index, at), None)


def in_plane(bold, edge, side):
    cells_x, cells_y, cells_z, frames = bold.shape
    group = 256 // cells_z
    band = np.zeros((cells_z, cells_z), np.float64)
    for k in range(-REACH, REACH + 1):
        band += kernel_taps[k + REACH] * np.eye(cells_z, k=k)
    band = np.kron(np.eye(group), band).astype(np.float32)
    high = band.astype(BF)
    low = (band - high.astype(np.float32)).astype(BF)
    lanes = 3 * LANES
    pieces = [jax.ShapeDtypeStruct((5, cells_x, pairs, cells_z, LANES), BF) for pairs in PAIRS]
    piece_specs = [pl.BlockSpec((5, 1) + piece.shape[2:], lambda x: (0, x, 0, 0, 0)) for piece in pieces]
    whole = pl.BlockSpec(high.shape, lambda x: (0, 0))
    outs = pl.pallas_call(
        functools.partial(in_plane_kernel, frames=frames),
        grid=(cells_x,),
        in_specs=[
            pl.BlockSpec(memory_space=pltpu.SMEM),
            pl.BlockSpec((1, cells_y, cells_z, lanes), lambda x: (x, 0, 0, 0)),
            pl.BlockSpec((1, REACH, cells_z, lanes), lambda x: (x, 0, 0, 0)),
            whole,
            whole,
        ],
        out_specs=piece_specs * 2,
        out_shape=pieces * 2,
        scratch_shapes=[pltpu.VMEM((cells_y + 2 * REACH, cells_z, lanes), F32)],
        compiler_params=pltpu.CompilerParams(vmem_limit_bytes=VMEM),
        name="in_plane",
    )(side, bold, edge, jnp.asarray(high), jnp.asarray(low))
    return outs[:NCHUNK], outs[NCHUNK:]


def rank_kernel(row_ref, out_ref, turns_ref, *, column):
    seeds, chips = row_ref.shape[1], out_ref.shape[0]
    seed = row_ref[...]
    chip = lax.broadcasted_iota(jnp.int32, (chips, 1), 0) * column
    here = jnp.where((seed >= chip) & (seed < chip + column), 1.0, 0.0)
    earlier = lax.broadcasted_iota(jnp.int32, (seeds, seeds), 0) < lax.broadcasted_iota(jnp.int32, (seeds, seeds), 1)
    before = dot(here.astype(BF), jnp.where(earlier, 1.0, 0.0).astype(BF))
    rank = jnp.sum(here * before, axis=0, keepdims=True)
    out_ref[...] = jnp.broadcast_to(rank.astype(jnp.int32), out_ref.shape)
    turns_ref[0] = (jnp.max(rank).astype(jnp.int32) + LIST) // LIST


def part_kernel(place_ref, row_ref, rank_ref, *refs, cells, column, strip):
    chunks, rests, outs = refs[:NCHUNK], refs[NCHUNK : 2 * NCHUNK], refs[2 * NCHUNK :]
    cells_x, cells_y, cells_z = cells
    brick, side, turn = place_ref[0], place_ref[1], place_ref[2]
    half = 3 * HALF
    slots = 2 * half
    seed = row_ref[...]
    rank = rank_ref[0:1] - turn * LIST
    spot = jnp.where((rank >= 0) & (rank < LIST), (seed // column) * LIST + rank, -1)
    slot = lax.broadcasted_iota(jnp.int32, (slots, 1), 0)
    core = jnp.where(slot < half, side, 1 - side)
    slot = jnp.where(slot < half, slot, slot - half)
    which = jnp.where(slot < HALF, 0, jnp.where(slot < 2 * HALF, 1, 2))
    want = (brick - 1 + which) * LIST + core * HALF + slot - which * HALF
    want = jnp.where(want >= 0, want, -2)
    found = jnp.sum(jnp.where(spot == want, (seed + 1).astype(F32), 0.0), axis=1, keepdims=True)
    found = found.astype(jnp.int32) - 1
    seed_x = found // strip
    within = found - seed_x * strip
    seed_y = within // cells_z
    seed_z = within - seed_y * cells_z
    from_x = seed_x - brick * cells_x
    from_y = jnp.where(found < 0, -1, seed_y - side * cells_y)

    main = jnp.zeros((slots, 2 * LANES), F32)
    last = jnp.zeros((2 * slots, LANES), F32)

    def product(weights, index, pieces):
        head, tail = (
            jnp.concatenate([refs[index][k].reshape(-1, LANES) for k in pieces], axis=1) for refs in (chunks, rests)
        )
        high, low = weights
        return dot(high, head) + dot(high, tail) + dot(low, head)

    for index, pairs in enumerate(PAIRS):
        lane = lax.broadcasted_iota(jnp.int32, (1, cells_x * pairs * cells_z), 1)
        shift_z, shift_p = cells_z.bit_length() - 1, pairs.bit_length() - 1
        row = 2 * (((lane >> shift_z) & (pairs - 1)) + sum(PAIRS[:index]))
        gap = ((lane >> (shift_z + shift_p)) - from_x).astype(F32)
        taps = jnp.where(jnp.abs(gap) <= REACH, jnp.exp(gap * gap * (-1.0 / 8.0)) * (1.0 / TAP_SUM), 0.0)
        taps = jnp.where((lane & (cells_z - 1)) == seed_z, taps, 0.0)
        both = [split(jnp.where(row + odd == from_y, taps, 0.0)) for odd in range(2)]
        main = main + product(both[0], index, (0, 1)) + product(both[1], index, (2, 3))
        last = last + product([jnp.concatenate(w, axis=0) for w in zip(*both)], index, (4,))
    near = lax.broadcasted_iota(jnp.int32, (1, LANES), 1) < LANES // 2
    last = jnp.where(near, last[:slots] + pltpu.roll(last[slots:], LANES // 2, 1), 0.0)
    for k, out_ref in enumerate(outs):
        out_ref[:, : 2 * LANES] = main[k * half : (k + 1) * half]
        out_ref[:, 2 * LANES :] = last[k * half : (k + 1) * half]


def sum_kernel(own_ref, other_ref, *outs):
    for k, out_ref in enumerate(outs):
        rows = slice(k * HALF, (k + 1) * HALF)
        out_ref[...] = own_ref[rows] + other_ref[rows]


def scale_kernel(*refs, frames):
    ins, out_ref = refs[:-1], refs[-1]
    total = ins[0][...]
    for ref in ins[1:]:
        total = total + ref[...]
    var = jnp.sum(total * total, axis=1, keepdims=True) * (1.0 / frames)
    total = total * lax.rsqrt(var + 1e-06)
    half = HALF // 2
    first, second = total[:half], total[half:]
    last = first[:, 2 * LANES :] + pltpu.roll(second[:, 2 * LANES :], LANES // 2, 1)
    pieces = (first[:, :LANES], first[:, LANES : 2 * LANES], second[:, :LANES], second[:, LANES : 2 * LANES], last)
    for k, piece in enumerate(pieces):
        out_ref[0, k] = piece.astype(BF)


def order_kernel(place_ref, row_ref, rank_ref, own_ref, other_ref, out_ref, *, column):
    side, turn = place_ref[1], place_ref[2]
    half = HALF // 2
    count = own_ref.shape[0] * half
    rank = rank_ref[0:1] - turn * LIST
    quarter = sum(jnp.where(rank >= k * half, 1, 0) for k in range(1, 4))
    part = jnp.where(side == 0, quarter, jnp.where(quarter < 2, quarter + 2, quarter - 2))
    spot = part * count + (row_ref[...] // column) * half + rank - quarter * half
    spot = jnp.where((rank >= 0) & (rank < LIST), spot, -1)
    slot = lax.broadcasted_iota(jnp.int32, (count, 1), 0)
    picks = [jnp.where(spot - part * count == slot, 1.0, 0.0).astype(BF) for part in range(4)]

    def piece(part, k):
        ref = (own_ref, other_ref)[part // 2]
        return dot(ref[:, k].reshape(count, LANES), picks[part], (((0,), (0,)), ((), ())))

    for k in range(2):
        value = piece(0, k) + piece(1, 2 + k) + piece(2, k) + piece(3, 2 + k)
        out_ref[k * LANES : (k + 1) * LANES] = value.astype(BF)
    even, odd = piece(0, 4) + piece(2, 4), piece(1, 4) + piece(3, 4)
    last = even[: LANES // 2] + odd[LANES // 2 :]
    out_ref[2 * LANES :] = jnp.concatenate([last, jnp.zeros_like(last)], axis=0).astype(BF)


def in_order(place, row, ranks, own, other, column):
    seeds, block = row.shape[1], 256
    return pl.pallas_call(
        functools.partial(order_kernel, column=column),
        grid=(seeds // block,),
        in_specs=[
            pl.BlockSpec(memory_space=pltpu.SMEM),
            pl.BlockSpec((1, block), lambda i: (0, i)),
            pl.BlockSpec((ranks.shape[0], block), lambda i: (0, i)),
        ]
        + [pl.BlockSpec(own.shape, lambda i: (0, 0, 0, 0))] * 2,
        out_specs=pl.BlockSpec((3 * LANES, block), lambda i: (0, i)),
        out_shape=jax.ShapeDtypeStruct((3 * LANES, seeds), BF),
        compiler_params=pltpu.CompilerParams(vmem_limit_bytes=VMEM),
        name="order",
    )(place, row, ranks, own, other)


def finish_kernel(bounds_ref, table_ref, own_ref, before_ref, after_ref, *refs, frames, first):
    out_ref = refs[-1]
    cells_x, cells_z = own_ref.shape[1], own_ref.shape[3]
    pair = first + pl.program_id(0)
    near = lax.broadcasted_iota(jnp.int32, (1, LANES), 1) < LANES // 2
    depth = lax.broadcasted_iota(jnp.int32, (cells_z, 1), 0)
    table = table_ref[...]

    def plane(k, x):
        if x < 0:
            return before_ref[k, x + cells_x, 0].astype(F32)
        if x >= cells_x:
            return after_ref[k, x - cells_x, 0].astype(F32)
        return own_ref[k, x, 0].astype(F32)

    rows = []
    for x in range(cells_x):
        sums = []
        for k in range(5):
            total = kernel_taps[REACH] * plane(k, x)
            for t in range(1, REACH + 1):
                total = total + kernel_taps[REACH + t] * (plane(k, x - t) + plane(k, x + t))
            sums.append(total)
        for odd in range(2):
            last = pltpu.roll(sums[4], LANES // 2, 1) if odd else sums[4]
            pieces = (sums[2 * odd], sums[2 * odd + 1], jnp.where(near, last, 0.0))
            square = pieces[0] * pieces[0] + pieces[1] * pieces[1] + pieces[2] * pieces[2]
            var = jnp.sum(square, axis=1, keepdims=True) * (1.0 / frames)
            row = x * (bounds_ref.shape[1] // cells_x) + 2 * pair + odd
            inside = (depth >= bounds_ref[0, row]) & (depth < bounds_ref[1, row])
            scale = jnp.where(inside, lax.rsqrt(var + 1e-06), 0.0)
            rows.append(jnp.concatenate([(p * scale).astype(BF) for p in pieces], axis=1))
    corr = dot(jnp.concatenate(rows, axis=0), table) * (1.0 / frames)
    out_ref[...] = corr.astype(BF).reshape(out_ref.shape)


def finish(bounds, table, own, before, after, out, shape, frames, chunk):
    _, cells_x, pairs, cells_z, _ = own.shape
    first = sum(PAIRS[:chunk])
    spec = pl.BlockSpec((5, cells_x, 1, cells_z, LANES), lambda p: (0, 0, p, 0, 0))
    more = [] if out is None else [out]
    return pl.pallas_call(
        functools.partial(finish_kernel, frames=frames, first=first),
        grid=(pairs,),
        in_specs=[
            pl.BlockSpec(memory_space=pltpu.SMEM),
            pl.BlockSpec(table.shape, lambda p: (0, 0)),
            spec,
            spec,
            spec,
        ]
        + [pl.BlockSpec(memory_space=pl.ANY)] * len(more),
        out_specs=pl.BlockSpec((cells_x, 2, cells_z, shape[-1]), lambda p: (0, first + p, 0, 0)),
        out_shape=jax.ShapeDtypeStruct(shape, BF),
        input_output_aliases={5: 0} if more else {},
        compiler_params=pltpu.CompilerParams(vmem_limit_bytes=VMEM),
        name="finish",
    )(bounds, table, own, before, after, *more)


def call(kernel, out, *args, smem=0):
    in_specs = [pl.BlockSpec(memory_space=pltpu.SMEM)] * smem + [pl.BlockSpec(memory_space=pltpu.VMEM)] * (len(args) - smem)
    multi = isinstance(out, list)
    return pl.pallas_call(
        kernel,
        in_specs=in_specs,
        out_specs=[pl.BlockSpec(memory_space=pltpu.VMEM)] * len(out) if multi else pl.BlockSpec(memory_space=pltpu.VMEM),
        out_shape=out,
        compiler_params=pltpu.CompilerParams(vmem_limit_bytes=VMEM),
    )(*args)


def shift(value, step, flip=False, wrap=False):
    size, cores = lax.axis_size("gx"), lax.axis_size("gy")
    pairs = []
    for i in range(size):
        if wrap or 0 <= i + step < size:
            for c in range(cores):
                source = (i + step) % size * cores + (cores - 1 - c if flip else c)
                pairs.append((source, i * cores + c))
    return lax.ppermute(value, ("gx", "gy"), pairs)


def local(bold, brain_bounds, seed_index):
    frames, cells_x, cells_y, cells_z = bold.shape
    seeds = seed_index.shape[0]
    size, cores = lax.axis_size("gx"), lax.axis_size("gy")
    brick, side = lax.axis_index("gx"), lax.axis_index("gy")
    bold = jnp.transpose(bold, (1, 2, 3, 0))
    sides = side.astype(jnp.int32).reshape(1)

    send = lax.dynamic_slice_in_dim(bold, jnp.where(side == 0, cells_y - REACH, 0), REACH, axis=1)
    edge = shift(send, 0, flip=True)
    bounds = jnp.transpose(brain_bounds, (2, 0, 1)).reshape(2, cells_x * cells_y)
    edge, bounds = lax.optimization_barrier((edge, bounds))
    chunks, rests = in_plane(bold, edge, sides)
    halos = [(shift(c, -1), shift(c, 1)) for c in chunks]

    strip = cores * cells_y * cells_z
    column = cells_x * strip
    row = seed_index.reshape(1, seeds)
    ranks, turns = pl.pallas_call(
        functools.partial(rank_kernel, column=column),
        in_specs=[pl.BlockSpec(memory_space=pltpu.VMEM)],
        out_specs=[pl.BlockSpec(memory_space=pltpu.VMEM), pl.BlockSpec(memory_space=pltpu.SMEM)],
        out_shape=[jax.ShapeDtypeStruct((size, seeds), jnp.int32), jax.ShapeDtypeStruct((1,), jnp.int32)],
        name="rank",
    )(row)

    def table_of(turn):
        place = jnp.stack([brick, side, turn]).astype(jnp.int32)
        own, other = call(
            functools.partial(part_kernel, cells=(cells_x, cells_y, cells_z), column=column, strip=strip),
            [jax.ShapeDtypeStruct((3 * HALF, 3 * LANES), F32)] * 2,
            place,
            row,
            ranks,
            *chunks,
            *rests,
            smem=1,
        )
        other = shift(other, 0, flip=True)
        lists = call(sum_kernel, [jax.ShapeDtypeStruct((HALF, 3 * LANES), F32)] * 3, own, other)
        below = shift(lists[2], -1)
        above = shift(lists[0], 1)
        mine = call(
            functools.partial(scale_kernel, frames=frames),
            jax.ShapeDtypeStruct((1, 5, HALF // 2, LANES), BF),
            lists[1],
            below,
            above,
        )
        every = lax.all_gather(mine, "gx", axis=0, tiled=True)
        other = shift(every, 0, flip=True)
        return in_order(place, row, ranks, every, other, column)

    table = table_of(jnp.int32(0))
    _, table = lax.while_loop(
        lambda s: s[0] < turns[0], lambda s: (s[0] + 1, s[1] + table_of(s[0])), (jnp.int32(1), table)
    )

    shape = (cells_x, cells_y, cells_z, seeds)
    out = None
    for index in range(NCHUNK):
        out = finish(bounds, table, chunks[index], *halos[index], out, shape, frames, index)
    return out


def solution(mesh):
    placed = (P("subj", "gx", "gy", None), P("gx", "gy", "subj"), P("subj"))

    return jax.shard_map(local, mesh=mesh, in_specs=placed, out_specs=P("gx", "gy", None, "subj"), check_vma=False)
```

time: 472 us -> 195 us (0.41)
  blocking collectives: 218 us -> 76.3 us
  waiting for transfers between devices: 133 us -> 40.5 us
  other arithmetic: 79.3 us -> 0.65 us
  Pallas kernels: 0 us -> 48.2 us
  local copies, waits for them, and re-layouts: 24.2 us -> 7.2 us
  starting transfers between devices: 10.8 us -> 20.1 us
  matrix products: 5.67 us -> 0 us
    psum x1 -> x0, blocking collectives: 218 us -> none  [local(): table = lax.psum(picked, ('gx', 'gy')).astype(jnp.bfloat16)]
    ppermute x4 -> x11, waiting for transfers between devices: 133 us -> 40.5 us  [shift(): return lax.ppermute(value, ('gx', 'gy'), pairs)]
    all_gather x0 -> x1, blocking collectives: none -> 76.3 us  [table_of(): every = lax.all_gather(mine, 'gx', axis=0, tiled=True)]
    pallas_call x0 -> x9, Pallas kernels: none -> 48.2 us  [the longest x3 20 us: finish(): pl.pallas_call(functools.partial(finish_kernel, frames=frames, first=firs...]
    add x2 -> x0, other arithmetic: 42.9 us -> none  [smooth_axis(): total + kernel_taps[k] * lax.slice_in_dim(padded, k, k + count, axis=axis)]
    reduce_sum x2 -> x0, other arithmetic: 27.7 us -> none  [the longest x1 24 us: local(): mean = jnp.mean(smoothed, axis=0)]
    concatenate x2 -> x0, local copies, waits for them, and re-layouts: 13.5 us -> none  [with_halo(): shard = jnp.concatenate([before, shard, after], axis=dim)]
    ppermute x4 -> x11, starting transfers between devices: 10.8 us -> 20.1 us  [shift(): return lax.ppermute(value, ('gx', 'gy'), pairs)]
  transfers between devices with their start and end apart: 4 -> 11, of which waited for: 3 -> 5; matrix products, arithmetic and copies ran while one was open for 2% -> 1% of each run, Pallas kernels for 0% -> 11%
where the time goes in v1:
time: 195 us; the launch traced here: 194 us
  blocking collectives  76.3 us (39%)
  Pallas kernels  48.2 us (25%)
  waiting for transfers between devices  40.5 us (21%)
  starting transfers between devices  20.1 us (10%)
  local copies, waits for them, and re-layouts  7.2 us (4%)
    all_gather x1, blocking collectives, table_of(): every = lax.all_gather(mine, 'gx', axis=0, tiled=True)  76.3 us
    ppermute x11, waiting for transfers between devices, shift(): return lax.ppermute(value, ('gx', 'gy'), pairs)  40.5 us
    ppermute x11, starting transfers between devices, shift(): return lax.ppermute(value, ('gx', 'gy'), pairs)  20.1 us
    pallas_call x3, Pallas kernels, finish(): pl.pallas_call(functools.partial(finish_kernel, frames=frames, first=firs...  20 us
    pallas_call x1, Pallas kernels, in_plane(): pl.pallas_call(functools.partial(in_plane_kernel, frames=frames), grid=(c...  13 us
    pallas_call x3, Pallas kernels, call(): pl.pallas_call(kernel, in_specs=in_specs, out_specs=[pl.BlockSpec(memory_...  9.22 us
    unnamed x18, local copies, waits for them, and re-layouts  4.71 us
    pallas_call x1, Pallas kernels, in_order(): pl.pallas_call(functools.partial(order_kernel, column=column), grid=(seed...  4.33 us
  transfers between devices with their start and end apart: 11, of which 5 were waited for; matrix products, arithmetic and copies ran while one was open for 1% of the time, Pallas kernels for 11%

profile of v1, /device:TPU:44, one launch (start us, length us, event | category | flops | bytes accessed | tf_op | source)
XLA Modules:
  0.0 193.9 jit_solution(8742196116166512530)
XLA Ops:
  0.0 0.0 copy-start.6
  0.0 1.2 dynamic-slice_bitcast_fusion
  1.2 0.1 collective-permute-start.4
  1.4 0.7 copy.9
  2.0 0.6 reshape.7.bounds_ref
  2.7 1.7 rank.1
  4.3 0.7 pad_add_fusion.1.place_ref
  5.0 0.0 collective-permute-done.4.edge_ref
  5.0 0.0 copy-start.5
  5.0 0.9 copy-done.5
  5.9 13.0 %in_plane.1 = (bf16[5,4,4,32,128]{4,3,2,1,0:T(8,128)(2,1)}, bf16[5,4,8,32,128]{4,3,2,1,0:T(8,128)(2,1)}, bf16[5,4,4,32,128]{4,3,2,1,0:T(8,128)(2,1)S(1)}, bf16[5...) custom-call(s32[1]{0:T(128)} %bitcast.7.side_ref, ...), custom_call_target="tpu_custom_call" | custom-call | tf_op jit(solution)/shard_map/in_plane/pallas_call | solution.py:94
  18.9 0.0 copy-done.6
  18.9 6.0 %shard_map.55 = (f32[96,384]{1,0:T(8,128)}, f32[96,384]{1,0:T(8,128)}) custom-call(s32[3]{0:T(128)} %pad_add_fusion.1.place_ref, s32[1,1024]{1,0:T(1,128)S(1)} %bitcast.20, s32[32,1024]{1,0:T(8,128)S(1)} %get-tuple-element.231.rank_ref, bf16[5,4,4,32,128]{4,3,2,1,0:T(8,128)(2,1)} %get-tuple-element.232.refs_0_.own_ref, ...), custom_call_target="tpu_custom_call" | custom-call | tf_op jit(solution)/shard_map/pallas_call | solution.py:302
  24.8 0.5 collective-permute-start.5
  25.3 1.2 collective-permute-done.5.other_ref
  26.5 0.0 copy-start.10
  26.5 0.7 copy-done.10
  27.2 1.6 shard_map.56
  28.8 4.0 %collective-permute-start.6 = (f32[32,384]{1,0:T(8,128)}, f32[32,384]{1,0:T(8,128)S(1)}, u32[]{:S(2)}, u32[]{:S(2)}) collective-permute-start(f32[32,384]{1,0:T(8,128)} %get-tuple-element.105), channel_id=1, source_target_pairs={{0,2},{1,3},{2,4},{3,5},{4,6},{5,7},{6,8},{7,9},{8,10},{9,11},{10,... | collective-permute-start | bytes 147464 | tf_op jit(solution)/shard_map/ppermute | solution.py:319
  32.9 1.3 collective-permute-start.7
  34.2 0.7 collective-permute-done.6.refs_1_
  34.9 0.0 copy-start.11
  34.9 4.3 %collective-permute-done.7.refs_2_ = f32[32,384]{1,0:T(8,128)S(1)} collective-permute-done((f32[32,384]{1,0:T(8,128)}, f32[32,384]{1,0:T(8,128)S(1)}, u32[]{:S(2)}, u32[]{:S(2)}) %collective-permute-start.7) | collective-permute-done | bytes 49184 | tf_op jit(solution)/shard_map/ppermute | solution.py:319
  39.2 0.0 copy-start.12
  39.2 0.0 copy-done.11
  39.2 0.6 copy-done.12
  39.8 1.6 shard_map.57
  41.4 76.3 %all_gather.6.own_ref = bf16[32,5,16,128]{3,2,1,0:T(8,128)(2,1)S(1)} all-gather(bf16[1,5,16,128]{3,2,1,0:T(8,128)(2,1)} %shard_map.57), channel_id=1, replica_groups=mesh['subj'=4,'gx'=32,'gy'=2] {'gx'}, dimensions={0}, use_global_device_ids=true | all-gather | bytes 675840 | tf_op jit(solution)/shard_map/all_gather | solution.py:371
  117.7 0.0 copy-start.2
  117.7 0.0 collective-permute-start.8
  117.7 3.0 %collective-permute-start.13 = (bf16[5,4,4,32,128]{4,3,2,1,0:T(8,128)(2,1)}, bf16[5,4,4,32,128]{4,3,2,1,0:T(8,128)(2,1)}, u32[]{:S(2)}, u32[]{:S(2)}) collective-permute-start(bf16[5,4,4,32,128]{4,3,2,1,0:T(8,128)(2,1)} %get-tuple-element.232.refs_0_.own_ref), channel_id=1, source_target_pairs={{0,2},{1,3},{2,4},{3,5},{4,6},{5,7},{6,8},{7,9},{8,10},{9,11},{10,... | collective-permute-start | bytes 1966088 | tf_op jit(solution)/shard_map/ppermute | solution.py:319
  120.7 2.8 %collective-permute-start.11 = (bf16[5,4,8,32,128]{4,3,2,1,0:T(8,128)(2,1)}, bf16[5,4,8,32,128]{4,3,2,1,0:T(8,128)(2,1)}, u32[]{:S(2)}, u32[]{:S(2)}) collective-permute-start(bf16[5,4,8,32,128]{4,3,2,1,0:T(8,128)(2,1)} %get-tuple-element.233.refs_1_.own_ref), channel_id=1, source_target_pairs={{0,2},{1,3},{2,4},{3,5},{4,6},{5,7},{6,8},{7,9},{8,10},{9,11},{10,... | collective-permute-start | bytes 3932168 | tf_op jit(solution)/shard_map/ppermute | solution.py:319
  123.5 1.3 collective-permute-start.12
  124.8 0.0 collective-permute-done.8.other_ref
  124.8 0.0 copy-done.2
  124.8 4.3 %order.2 = bf16[384,1024]{1,0:T(8,128)(2,1)S(1)} custom-call(s32[3]{0:T(128)} %pad_add_fusion.1.place_ref, s32[1,1024]{1,0:T(1,128)S(1)} %bitcast.21, s32[32,1024]{1,0:T(8,128)S(1)} %get-tuple-element.231.rank_ref, bf16[32,5,16,128]{3,2,1,0:T(8,128)(2,1)} %copy-done.2, bf16[32,5,16,128]{3,2,1,0:T(8,128)(2,1)} %collective-permute-done.8.other_ref), custom_call_target="tpu_custom_call" | custom-call | tf_op jit(solution)/shard_map/order/pallas_call | solution.py:223
  129.2 0.8 while.10
  130.0 1.3 collective-permute-start.14
  131.3 1.3 collective-permute-start.10
  132.6 2.7 %collective-permute-done.13.before_ref = bf16[5,4,4,32,128]{4,3,2,1,0:T(8,128)(2,1)} collective-permute-done((bf16[5,4,4,32,128]{4,3,2,1,0:T(8,128)(2,1)}, bf16[5,4,4,32,128]{4,3,2,1,0:T(8,128)(2,1)}, u32[]{:S(2)}, u32[]{:S(2)}) %collective-permute-start.13) | collective-permute-done | bytes 655392 | tf_op jit(solution)/shard_map/ppermute | solution.py:319
  135.3 4.4 %collective-permute-start.9 = (bf16[5,4,4,32,128]{4,3,2,1,0:T(8,128)(2,1)S(1)}, bf16[5,4,4,32,128]{4,3,2,1,0:T(8,128)(2,1)S(1)}, u32[]{:S(2)}, u32[]{:S(2)}) collective-permute-start(bf16[5,4,4,32,128]{4,3,2,1,0:T(8,128)(2,1)S(1)} %get-tuple-element.268), channel_id=1, source_target_pairs={{0,2},{1,3},{2,4},{3,5},{4,6},{5,7},{6,8},{7,9},{8,10},{9,11},{10,... | collective-permute-start | bytes 1966088 | tf_op jit(solution)/shard_map/ppermute | solution.py:319
  139.8 31.6 %collective-permute-done.14.after_ref = bf16[5,4,4,32,128]{4,3,2,1,0:T(8,128)(2,1)S(1)} collective-permute-done((bf16[5,4,4,32,128]{4,3,2,1,0:T(8,128)(2,1)}, bf16[5,4,4,32,128]{4,3,2,1,0:T(8,128)(2,1)S(1)}, u32[]{:S(2)}, u32[]{:S(2)}) %collective-permute-start.14) | collective-permute-done | bytes 655392 | tf_op jit(solution)/shard_map/ppermute | solution.py:319
  171.3 0.0 copy-start.9
  171.3 0.9 copy-done.9
  172.2 5.3 %finish.3.refs_0_ = bf16[4,32,32,1024]{3,2,1,0:T(8,128)(2,1)} custom-call(s32[2,128]{1,0:T(2,128)} %reshape.7.bounds_ref, bf16[384,1024]{1,0:T(8,128)(2,1)S(1)} %get-tuple-element.108.table_ref, bf16[5,4,4,32,128]{4,3,2,1,0:T(8,128)(2,1)} %get-tuple-element.232.refs_0_.own_ref, bf16[5,4,4,32,128]{4,3,2,1,0:T(8,128)(2,1)} %collective-permute-done.13.before_ref, ...), custom_call_target="tpu_custom_call" | custom-call | tf_op jit(solution)/shard_map/finish/pallas_call | solution.py:280
  177.5 0.0 collective-permute-done.11.before_ref
  177.5 0.0 collective-permute-done.12.after_ref
  177.5 9.4 %finish.4.refs_0_ = bf16[4,32,32,1024]{3,2,1,0:T(8,128)(2,1)} custom-call(s32[2,128]{1,0:T(2,128)} %reshape.7.bounds_ref, bf16[384,1024]{1,0:T(8,128)(2,1)S(1)} %get-tuple-element.108.table_ref, bf16[5,4,8,32,128]{4,3,2,1,0:T(8,128)(2,1)} %get-tuple-element.233.refs_1_.own_ref, ...), custom_call_target="tpu_custom_call", output_to_operand_aliasing={{}: (5, {})} | custom-call | tf_op jit(solution)/shard_map/finish/pallas_call | solution.py:280
  187.0 0.0 collective-permute-done.10.after_ref
  187.0 0.0 copy-start.7
  187.0 0.0 collective-permute-done.9.before_ref
  187.0 0.9 copy-done.7
  187.8 0.0 copy-start.8
  187.8 0.8 copy-done.8
  188.7 5.2 %finish.5 = bf16[4,32,32,1024]{3,2,1,0:T(8,128)(2,1)} custom-call(s32[2,128]{1,0:T(2,128)} %reshape.7.bounds_ref, bf16[384,1024]{1,0:T(8,128)(2,1)S(1)} %get-tuple-element.108.table_ref, bf16[5,4,4,32,128]{4,3,2,1,0:T(8,128)(2,1)S(1)} %get-tuple-element.268, bf16[5,4,4,32,128]{4,3,2,1,0:T(8,128)(2,1)} %copy-done.8, ...), custom_call_target="tpu_custom_call", output_to_operand_aliasing={{}: (5, {})} | custom-call | tf_op jit(solution)/shard_map/finish/pallas_call | solution.py:280
Async XLA Ops:
  0.0 18.9 %copy-start.6 = (s32[1024]{0:T(1024)S(1)}, s32[1024]{0:T(1024)}, u32[]{:S(2)}) copy-start(s32[1024]{0:T(1024)} %param.9) | copy-start | bytes 12292
  1.2 3.8 %collective-permute-start.4 = (f32[4,4,32,300]{3,2,1,0:T(8,128)S(1)}, f32[4,4,32,300]{3,2,1,0:T(8,128)S(1)}, u32[]{:S(2)}, u32[]{:S(2)}) collective-permute-start(f32[4,4,32,300]{3,2,1,0:T(8,128)S(1)} %dynamic-slice_bitcast_fusion), channel_id=1, source_target_pairs={{1,0},{0,1},{3,2},{2,3},{5,4},{4,5},{7,6},{6,7},{9,8},{8,9},{11,10... | collective-permute-start | bytes 1843208 | tf_op jit(solution)/shard_map/ppermute | solution.py:319
  5.0 0.9 copy-start.5
  24.8 1.7 collective-permute-start.5
  26.5 0.7 copy-start.10
  28.8 6.1 %collective-permute-start.6 = (f32[32,384]{1,0:T(8,128)}, f32[32,384]{1,0:T(8,128)S(1)}, u32[]{:S(2)}, u32[]{:S(2)}) collective-permute-start(f32[32,384]{1,0:T(8,128)} %get-tuple-element.105), channel_id=1, source_target_pairs={{0,2},{1,3},{2,4},{3,5},{4,6},{5,7},{6,8},{7,9},{8,10},{9,11},{10,... | collective-permute-start | bytes 147464 | tf_op jit(solution)/shard_map/ppermute | solution.py:319
  32.9 6.3 %collective-permute-start.7 = (f32[32,384]{1,0:T(8,128)}, f32[32,384]{1,0:T(8,128)S(1)}, u32[]{:S(2)}, u32[]{:S(2)}) collective-permute-start(f32[32,384]{1,0:T(8,128)} %get-tuple-element.106), channel_id=1, source_target_pairs={{2,0},{3,1},{4,2},{5,3},{6,4},{7,5},{8,6},{9,7},{10,8},{11,9},{12,... | collective-permute-start | bytes 147464 | tf_op jit(solution)/shard_map/ppermute | solution.py:319
  34.9 4.3 %copy-start.11 = (f32[32,384]{1,0:T(8,128)}, f32[32,384]{1,0:T(8,128)S(1)}, u32[]{:S(2)}) copy-start(f32[32,384]{1,0:T(8,128)S(1)} %collective-permute-done.6.refs_1_) | copy-start | bytes 147460
  39.2 0.6 copy-start.12
  117.7 7.1 %copy-start.2 = (bf16[32,5,16,128]{3,2,1,0:T(8,128)(2,1)}, bf16[32,5,16,128]{3,2,1,0:T(8,128)(2,1)S(1)}, u32[]{:S(2)}) copy-start(bf16[32,5,16,128]{3,2,1,0:T(8,128)(2,1)S(1)} %all_gather.6.own_ref) | copy-start | bytes 1966084
  117.7 7.1 %collective-permute-start.8 = (bf16[32,5,16,128]{3,2,1,0:T(8,128)(2,1)S(1)}, bf16[32,5,16,128]{3,2,1,0:T(8,128)(2,1)}, u32[]{:S(2)}, u32[]{:S(2)}) collective-permute-start(bf16[32,5,16,128]{3,2,1,0:T(8,128)(2,1)S(1)} %all_gather.6.own_ref), channel_id=1, source_target_pairs={{1,0},{0,1},{3,2},{2,3},{5,4},{4,5},{7,6},{6,7},{9,8},{8,9},{11,10... | collective-permute-start | bytes 1966088 | tf_op jit(solution)/shard_map/ppermute | solution.py:319
  117.7 17.6 %collective-permute-start.13 = (bf16[5,4,4,32,128]{4,3,2,1,0:T(8,128)(2,1)}, bf16[5,4,4,32,128]{4,3,2,1,0:T(8,128)(2,1)}, u32[]{:S(2)}, u32[]{:S(2)}) collective-permute-start(bf16[5,4,4,32,128]{4,3,2,1,0:T(8,128)(2,1)} %get-tuple-element.232.refs_0_.own_ref), channel_id=1, source_target_pairs={{0,2},{1,3},{2,4},{3,5},{4,6},{5,7},{6,8},{7,9},{8,10},{9,11},{10,... | collective-permute-start | bytes 1966088 | tf_op jit(solution)/shard_map/ppermute | solution.py:319
  120.7 56.8 %collective-permute-start.11 = (bf16[5,4,8,32,128]{4,3,2,1,0:T(8,128)(2,1)}, bf16[5,4,8,32,128]{4,3,2,1,0:T(8,128)(2,1)}, u32[]{:S(2)}, u32[]{:S(2)}) collective-permute-start(bf16[5,4,8,32,128]{4,3,2,1,0:T(8,128)(2,1)} %get-tuple-element.233.refs_1_.own_ref), channel_id=1, source_target_pairs={{0,2},{1,3},{2,4},{3,5},{4,6},{5,7},{6,8},{7,9},{8,10},{9,11},{10,... | collective-permute-start | bytes 3932168 | tf_op jit(solution)/shard_map/ppermute | solution.py:319
  123.5 54.0 %collective-permute-start.12 = (bf16[5,4,8,32,128]{4,3,2,1,0:T(8,128)(2,1)}, bf16[5,4,8,32,128]{4,3,2,1,0:T(8,128)(2,1)}, u32[]{:S(2)}, u32[]{:S(2)}) collective-permute-start(bf16[5,4,8,32,128]{4,3,2,1,0:T(8,128)(2,1)} %get-tuple-element.233.refs_1_.own_ref), channel_id=1, source_target_pairs={{2,0},{3,1},{4,2},{5,3},{6,4},{7,5},{8,6},{9,7},{10,8},{11,9},{12,... | collective-permute-start | bytes 3932168 | tf_op jit(solution)/shard_map/ppermute | solution.py:319
  130.0 41.3 %collective-permute-start.14 = (bf16[5,4,4,32,128]{4,3,2,1,0:T(8,128)(2,1)}, bf16[5,4,4,32,128]{4,3,2,1,0:T(8,128)(2,1)S(1)}, u32[]{:S(2)}, u32[]{:S(2)}) collective-permute-start(bf16[5,4,4,32,128]{4,3,2,1,0:T(8,128)(2,1)} %get-tuple-element.232.refs_0_.own_ref), channel_id=1, source_target_pairs={{2,0},{3,1},{4,2},{5,3},{6,4},{7,5},{8,6},{9,7},{10,8},{11,9},{12,... | collective-permute-start | bytes 1966088 | tf_op jit(solution)/shard_map/ppermute | solution.py:319
  131.3 55.7 %collective-permute-start.10 = (bf16[5,4,4,32,128]{4,3,2,1,0:T(8,128)(2,1)S(1)}, bf16[5,4,4,32,128]{4,3,2,1,0:T(8,128)(2,1)S(1)}, u32[]{:S(2)}, u32[]{:S(2)}) collective-permute-start(bf16[5,4,4,32,128]{4,3,2,1,0:T(8,128)(2,1)S(1)} %get-tuple-element.268), channel_id=1, source_target_pairs={{2,0},{3,1},{4,2},{5,3},{6,4},{7,5},{8,6},{9,7},{10,8},{11,9},{12,... | collective-permute-start | bytes 1966088 | tf_op jit(solution)/shard_map/ppermute | solution.py:319
  135.3 51.7 %collective-permute-start.9 = (bf16[5,4,4,32,128]{4,3,2,1,0:T(8,128)(2,1)S(1)}, bf16[5,4,4,32,128]{4,3,2,1,0:T(8,128)(2,1)S(1)}, u32[]{:S(2)}, u32[]{:S(2)}) collective-permute-start(bf16[5,4,4,32,128]{4,3,2,1,0:T(8,128)(2,1)S(1)} %get-tuple-element.268), channel_id=1, source_target_pairs={{0,2},{1,3},{2,4},{3,5},{4,6},{5,7},{6,8},{7,9},{8,10},{9,11},{10,... | collective-permute-start | bytes 1966088 | tf_op jit(solution)/shard_map/ppermute | solution.py:319
  171.3 0.9 copy-start.9
  187.0 0.9 copy-start.7
  187.8 0.8 copy-start.8

commit v2 on v1

--- a/solution.py
+++ b/solution.py
@@ -17,7 +17,7 @@
 LANES = 128
 BF = jnp.bfloat16
 F32 = jnp.float32
-PAIRS = (4, 8, 4)
+PAIRS = (4, 4, 4, 4)
 NCHUNK = len(PAIRS)
 HALF = 32
 LIST = 2 * HALF
@@ -51,8 +51,12 @@
         th, tl = taps_high[:size, :size], taps_low[:size, :size]
         return (dot(th, head) + dot(th, rest) + dot(tl, head)).reshape(count, cells_z, lanes)
 
-    for at in range(0, rows, group):
-        wide[REACH + at : REACH + at + group] = along_z(bold_ref[0, at : at + group], group)
+    def two_groups(step, _):
+        for k in range(2):
+            at = (2 * step + k) * group
+            wide[pl.ds(REACH + at, group)] = along_z(bold_ref[0, pl.ds(at, group)], group)
+
+    lax.fori_loop(0, rows // group // 2, two_groups, None)
     edge = along_z(edge_ref[0], REACH)
     wide[:REACH] = jnp.where(side == 1, edge, 0.0)
     wide[REACH + rows :] = jnp.where(side == 1, 0.0, edge)
@@ -191,7 +195,20 @@
     last = first[:, 2 * LANES :] + pltpu.roll(second[:, 2 * LANES :], LANES // 2, 1)
     pieces = (first[:, :LANES], first[:, LANES : 2 * LANES], second[:, :LANES], second[:, LANES : 2 * LANES], last)
     for k, piece in enumerate(pieces):
-        out_ref[0, k] = piece.astype(BF)
+        out_ref[k] = piece.astype(BF)
+
+
+def join_kernel(*refs):
+    out_ref = refs[-1]
+    count = out_ref.shape[0] // (len(refs) - 1)
+    for k, ref in enumerate(refs[:-1]):
+        out_ref[k * count : (k + 1) * count] = ref[...].reshape((count,) + out_ref.shape[1:])
+
+
+def join(pieces):
+    count = pieces[0].size // math.prod(pieces[0].shape[-3:])
+    shape = (count * len(pieces),) + pieces[0].shape[-3:]
+    return call(join_kernel, jax.ShapeDtypeStruct(shape, pieces[0].dtype), *pieces)
 
 
 def order_kernel(place_ref, row_ref, rank_ref, own_ref, other_ref, out_ref, *, column):
@@ -201,7 +218,15 @@
     rank = rank_ref[0:1] - turn * LIST
     quarter = sum(jnp.where(rank >= k * half, 1, 0) for k in range(1, 4))
     part = jnp.where(side == 0, quarter, jnp.where(quarter < 2, quarter + 2, quarter - 2))
-    spot = part * count + (row_ref[...] // column) * half + rank - quarter * half
+    size = own_ref.shape[0]
+    fourth = size // 4
+    ahead = row_ref[...] // column - place_ref[0]
+    ahead = jnp.where(ahead < 0, ahead + size, ahead)
+    far = ahead // fourth
+    low = ahead - far * fourth
+    far = jnp.where(2 * low > fourth, far + 1, far)
+    block = low * 4 + jnp.where(far >= 4, far - 4, far)
+    spot = part * count + block * half + rank - quarter * half
     spot = jnp.where((rank >= 0) & (rank < LIST), spot, -1)
     slot = lax.broadcasted_iota(jnp.int32, (count, 1), 0)
     picks = [jnp.where(spot - part * count == slot, 1.0, 0.0).astype(BF) for part in range(4)]
@@ -219,7 +244,7 @@
 
 
 def in_order(place, row, ranks, own, other, column):
-    seeds, block = row.shape[1], 256
+    seeds, block = row.shape[1], 128
     return pl.pallas_call(
         functools.partial(order_kernel, column=column),
         grid=(seeds // block,),
@@ -236,13 +261,11 @@
     )(place, row, ranks, own, other)
 
 
-def finish_kernel(bounds_ref, table_ref, own_ref, before_ref, after_ref, *refs, frames, first):
-    out_ref = refs[-1]
+def scores_kernel(bounds_ref, own_ref, before_ref, after_ref, out_ref, *, frames, first):
     cells_x, cells_z = own_ref.shape[1], own_ref.shape[3]
     pair = first + pl.program_id(0)
     near = lax.broadcasted_iota(jnp.int32, (1, LANES), 1) < LANES // 2
     depth = lax.broadcasted_iota(jnp.int32, (cells_z, 1), 0)
-    table = table_ref[...]
 
     def plane(k, x):
         if x < 0:
@@ -251,7 +274,6 @@
             return after_ref[k, x - cells_x, 0].astype(F32)
         return own_ref[k, x, 0].astype(F32)
 
-    rows = []
     for x in range(cells_x):
         sums = []
         for k in range(5):
@@ -267,33 +289,46 @@
             row = x * (bounds_ref.shape[1] // cells_x) + 2 * pair + odd
             inside = (depth >= bounds_ref[0, row]) & (depth < bounds_ref[1, row])
             scale = jnp.where(inside, lax.rsqrt(var + 1e-06), 0.0)
-            rows.append(jnp.concatenate([(p * scale).astype(BF) for p in pieces], axis=1))
-    corr = dot(jnp.concatenate(rows, axis=0), table) * (1.0 / frames)
+            for k, piece in enumerate(pieces):
+                out_ref[x, odd, :, k * LANES : (k + 1) * LANES] = (piece * scale).astype(BF)
+
+
+def scores(bounds, own, before, after, frames, index):
+    _, cells_x, pairs, cells_z, _ = own.shape
+    spec = pl.BlockSpec((5, cells_x, 1, cells_z, LANES), lambda p: (0, 0, p, 0, 0))
+    return pl.pallas_call(
+        functools.partial(scores_kernel, frames=frames, first=sum(PAIRS[:index])),
+        grid=(pairs,),
+        in_specs=[pl.BlockSpec(memory_space=pltpu.SMEM), spec, spec, spec],
+        out_specs=pl.BlockSpec((cells_x, 2, cells_z, 3 * LANES), lambda p: (0, p, 0, 0)),
+        out_shape=jax.ShapeDtypeStruct((cells_x, 2 * pairs, cells_z, 3 * LANES), BF),
+        name="scores",
+    )(bounds, own, before, after)
+
+
+def correlate_kernel(table_ref, score_ref, *refs, frames):
+    out_ref = refs[-1]
+    corr = dot(score_ref[...].reshape(-1, table_ref.shape[0]), table_ref[...]) * (1.0 / frames)
     out_ref[...] = corr.astype(BF).reshape(out_ref.shape)
 
 
-def finish(bounds, table, own, before, after, out, shape, frames, chunk):
-    _, cells_x, pairs, cells_z, _ = own.shape
-    first = sum(PAIRS[:chunk])
-    spec = pl.BlockSpec((5, cells_x, 1, cells_z, LANES), lambda p: (0, 0, p, 0, 0))
+def correlate(table, score, out, shape, frames, index):
+    cells_x, rows, cells_z, lanes = score.shape
+    first = sum(PAIRS[:index])
     more = [] if out is None else [out]
     return pl.pallas_call(
-        functools.partial(finish_kernel, frames=frames, first=first),
-        grid=(pairs,),
+        functools.partial(correlate_kernel, frames=frames),
+        grid=(rows // 2,),
         in_specs=[
-            pl.BlockSpec(memory_space=pltpu.SMEM),
             pl.BlockSpec(table.shape, lambda p: (0, 0)),
-            spec,
-            spec,
-            spec,
+            pl.BlockSpec((cells_x, 2, cells_z, lanes), lambda p: (0, p, 0, 0)),
         ]
         + [pl.BlockSpec(memory_space=pl.ANY)] * len(more),
         out_specs=pl.BlockSpec((cells_x, 2, cells_z, shape[-1]), lambda p: (0, first + p, 0, 0)),
         out_shape=jax.ShapeDtypeStruct(shape, BF),
-        input_output_aliases={5: 0} if more else {},
-        compiler_params=pltpu.CompilerParams(vmem_limit_bytes=VMEM),
-        name="finish",
-    )(bounds, table, own, before, after, *more)
+        input_output_aliases={2: 0} if more else {},
+        name="correlate",
+    )(table, score, *more)
 
 
 def call(kernel, out, *args, smem=0):
@@ -344,6 +379,10 @@
         out_shape=[jax.ShapeDtypeStruct((size, seeds), jnp.int32), jax.ShapeDtypeStruct((1,), jnp.int32)],
         name="rank",
     )(row)
+
+    fourth = size // 4
+    far_steps = [k * fourth for k in range(1, 4)]
+    near_steps = [k if 2 * k <= fourth else k - fourth for k in range(1, fourth)]
 
     def table_of(turn):
         place = jnp.stack([brick, side, turn]).astype(jnp.int32)
@@ -363,12 +402,15 @@
         above = shift(lists[0], 1)
         mine = call(
             functools.partial(scale_kernel, frames=frames),
-            jax.ShapeDtypeStruct((1, 5, HALF // 2, LANES), BF),
+            jax.ShapeDtypeStruct((5, HALF // 2, LANES), BF),
             lists[1],
             below,
             above,
         )
-        every = lax.all_gather(mine, "gx", axis=0, tiled=True)
+        far = [mine] + [shift(mine, step, wrap=True) for step in far_steps]
+        some = join(far)
+        near = [some] + [shift(some, step, wrap=True) for step in near_steps]
+        every = join(near)
         other = shift(every, 0, flip=True)
         return in_order(place, row, ranks, every, other, column)
 
@@ -380,7 +422,8 @@
     shape = (cells_x, cells_y, cells_z, seeds)
     out = None
     for index in range(NCHUNK):
-        out = finish(bounds, table, chunks[index], *halos[index], out, shape, frames, index)
+        score = scores(bounds, chunks[index], *halos[index], frames, index)
+        out = correlate(table, score, out, shape, frames, index)
     return out
 
 

time: 195 us -> 247 us (1.27)
  starting transfers between devices: 20.1 us -> 111 us
  blocking collectives: 76.3 us -> 0 us
  Pallas kernels: 48.2 us -> 67.8 us
  waiting for transfers between devices: 40.5 us -> 58.2 us
    ppermute x11 -> x23, starting transfers between devices: 20.1 us -> 111 us  [shift(): return lax.ppermute(value, ('gx', 'gy'), pairs)]
    all_gather x1 -> x0, blocking collectives: 76.3 us -> none  [table_of(): every = lax.all_gather(mine, 'gx', axis=0, tiled=True)]
    ppermute x11 -> x23, waiting for transfers between devices: 40.5 us -> 58.2 us  [shift(): return lax.ppermute(value, ('gx', 'gy'), pairs)]
    pallas_call x3 -> x8, Pallas kernels: 20 us -> 33.7 us  [the longest x4 17.4 us: correlate(): pl.pallas_call(functools.partial(correlate_kernel, frames=frames), grid=(...]
    pallas_call x3 -> x5, Pallas kernels: 9.22 us -> 11.4 us  [call(): pl.pallas_call(kernel, in_specs=in_specs, out_specs=[pl.BlockSpec(memory_...]
  transfers between devices with their start and end apart: 11 -> 23, of which waited for: 5 -> 11; matrix products, arithmetic and copies ran while one was open for 1% -> 1% of each run, Pallas kernels for 11% -> 9%
where the time goes in v2:
time: 247 us; the launch traced here: 244 us
  starting transfers between devices  111 us (45%)
  Pallas kernels  67.8 us (27%)
  waiting for transfers between devices  58.2 us (24%)
  local copies, waits for them, and re-layouts  6.16 us (2%)
    ppermute x23, starting transfers between devices, shift(): return lax.ppermute(value, ('gx', 'gy'), pairs)  111 us
    ppermute x23, waiting for transfers between devices, shift(): return lax.ppermute(value, ('gx', 'gy'), pairs)  58.2 us
    pallas_call x4, Pallas kernels, correlate(): pl.pallas_call(functools.partial(correlate_kernel, frames=frames), grid=(...  17.4 us
    pallas_call x4, Pallas kernels, scores(): pl.pallas_call(functools.partial(scores_kernel, frames=frames, first=sum(...  16.4 us
    pallas_call x1, Pallas kernels, in_plane(): pl.pallas_call(functools.partial(in_plane_kernel, frames=frames), grid=(c...  14.5 us
    pallas_call x5, Pallas kernels, call(): pl.pallas_call(kernel, in_specs=in_specs, out_specs=[pl.BlockSpec(memory_...  11.4 us
    pallas_call x1, Pallas kernels, in_order(): pl.pallas_call(functools.partial(order_kernel, column=column), grid=(seed...  6.57 us
  transfers between devices with their start and end apart: 23, of which 11 were waited for; matrix products, arithmetic and copies ran while one was open for 1% of the time, Pallas kernels for 9%

profile of v2, /device:TPU:44, one launch (start us, length us, event | category | flops | bytes accessed | tf_op | source)
XLA Modules:
  0.0 244.2 jit_solution(11766825142947878151)
XLA Ops:
  0.0 1.2 dynamic-slice_bitcast_fusion
  1.2 0.1 collective-permute-start.14
  1.4 0.7 copy.9
  2.1 0.6 reshape.8.bounds_ref
  2.7 1.7 rank.1
  4.4 0.6 pad_add_fusion.1.place_ref
  4.9 0.0 collective-permute-done.14.edge_ref
  4.9 0.9 copy-done.14
  5.8 14.5 %in_plane.1 = (bf16[5,4,4,32,128]{4,3,2,1,0:T(8,128)(2,1)S(1)}, bf16[5,4,4,32,128]{4,3,2,1,0:T(8,128)(2,1)S(1)}, bf16[5,4,4,32,128]{4,3,2,1,0:T(8,128)(2,1)S(1)}...) custom-call(s32[1]{0:T(128)} %bitcast.5.side_ref, ...), custom_call_target="tpu_custom_call" | custom-call | tf_op jit(solution)/shard_map/in_plane/pallas_call | solution.py:98
  20.3 4.6 %shard_map.55 = (f32[96,384]{1,0:T(8,128)}, f32[96,384]{1,0:T(8,128)}) custom-call(s32[3]{0:T(128)} %pad_add_fusion.1.place_ref, s32[1,1024]{1,0:T(1,128)S(1)} %bitcast.20, s32[32,1024]{1,0:T(8,128)S(1)} %get-tuple-element.261.rank_ref, bf16[5,4,4,32,128]{4,3,2,1,0:T(8,128)(2,1)S(1)} %get-tuple-element.262.refs_0_.own_ref, ...), custom_call_target="tpu_custom_call" | custom-call | tf_op jit(solution)/shard_map/pallas_call | solution.py:337
  25.0 0.5 collective-permute-start.15
  25.4 1.2 collective-permute-done.15.other_ref
  26.7 0.6 copy-done.23
  27.3 1.7 shard_map.56
  29.0 4.0 %collective-permute-start.16 = (f32[32,384]{1,0:T(8,128)}, f32[32,384]{1,0:T(8,128)S(1)}, u32[]{:S(2)}, u32[]{:S(2)}) collective-permute-start(f32[32,384]{1,0:T(8,128)} %get-tuple-element.118), channel_id=1, source_target_pairs={{0,2},{1,3},{2,4},{3,5},{4,6},{5,7},{6,8},{7,9},{8,10},{9,11},{10,... | collective-permute-start | bytes 147464 | tf_op jit(solution)/shard_map/ppermute | solution.py:354
  33.0 1.3 collective-permute-start.17
  34.3 4.7 %collective-permute-start.35 = (bf16[5,4,4,32,128]{4,3,2,1,0:T(8,128)(2,1)S(1)}, bf16[5,4,4,32,128]{4,3,2,1,0:T(8,128)(2,1)S(1)}, u32[]{:S(2)}, u32[]{:S(2)}) collective-permute-start(bf16[5,4,4,32,128]{4,3,2,1,0:T(8,128)(2,1)S(1)} %get-tuple-element.262.refs_0_.own_ref), channel_id=1, source_target_pairs={{0,2},{1,3},{2,4},{3,5},{4,6},{5,7},{6,8},{7,9},{8,10},{9,11},{10,... | collective-permute-start | bytes 1966088 | tf_op jit(solution)/shard_map/ppermute | solution.py:354
  39.1 1.3 collective-permute-start.36
  40.4 4.7 %collective-permute-start.33 = (bf16[5,4,4,32,128]{4,3,2,1,0:T(8,128)(2,1)S(1)}, bf16[5,4,4,32,128]{4,3,2,1,0:T(8,128)(2,1)S(1)}, u32[]{:S(2)}, u32[]{:S(2)}) collective-permute-start(bf16[5,4,4,32,128]{4,3,2,1,0:T(8,128)(2,1)S(1)} %get-tuple-element.263.refs_1_.own_ref), channel_id=1, source_target_pairs={{0,2},{1,3},{2,4},{3,5},{4,6},{5,7},{6,8},{7,9},{8,10},{9,11},{10,... | collective-permute-start | bytes 1966088 | tf_op jit(solution)/shard_map/ppermute | solution.py:354
  45.1 0.0 collective-permute-done.16.refs_1_
  45.1 0.0 copy-start.27
  45.1 1.3 collective-permute-start.34
  46.5 0.6 copy-done.28
  47.1 1.6 shard_map.57.refs_0_
  48.7 29.9 %collective-permute-start.18 = (bf16[5,16,128]{2,1,0:T(8,128)(2,1)}, bf16[5,16,128]{2,1,0:T(8,128)(2,1)S(1)}, u32[]{:S(2)}, u32[]{:S(2)}) collective-permute-start(bf16[5,16,128]{2,1,0:T(8,128)(2,1)} %shard_map.57.refs_0_), channel_id=1, source_target_pairs={{16,0},{17,1},{18,2},{19,3},{20,4},{21,5},{22,6},{23,7},{24,8},{25... | collective-permute-start | bytes 61448 | tf_op jit(solution)/shard_map/ppermute | solution.py:354
  78.5 9.1 %collective-permute-done.18.refs_1_ = bf16[5,16,128]{2,1,0:T(8,128)(2,1)S(1)} collective-permute-done((bf16[5,16,128]{2,1,0:T(8,128)(2,1)}, bf16[5,16,128]{2,1,0:T(8,128)(2,1)S(1)}, u32[]{:S(2)}, u32[]{:S(2)}) %collective-permute-start.18) | collective-permute-done | bytes 20512 | tf_op jit(solution)/shard_map/ppermute | solution.py:354
  87.7 21.3 %collective-permute-start.19 = (bf16[5,16,128]{2,1,0:T(8,128)(2,1)}, bf16[5,16,128]{2,1,0:T(8,128)(2,1)S(1)}, u32[]{:S(2)}, u32[]{:S(2)}) collective-permute-start(bf16[5,16,128]{2,1,0:T(8,128)(2,1)} %shard_map.57.refs_0_), channel_id=1, source_target_pairs={{32,0},{33,1},{34,2},{35,3},{36,4},{37,5},{38,6},{39,7},{40,8},{41... | collective-permute-start | bytes 61448 | tf_op jit(solution)/shard_map/ppermute | solution.py:354
  109.0 2.0 collective-permute-done.19.refs_2_
  111.0 16.7 %collective-permute-start.20 = (bf16[5,16,128]{2,1,0:T(8,128)(2,1)}, bf16[5,16,128]{2,1,0:T(8,128)(2,1)S(1)}, u32[]{:S(2)}, u32[]{:S(2)}) collective-permute-start(bf16[5,16,128]{2,1,0:T(8,128)(2,1)} %shard_map.57.refs_0_), channel_id=1, source_target_pairs={{48,0},{49,1},{50,2},{51,3},{52,4},{53,5},{54,6},{55,7},{56,8},{57... | collective-permute-start | bytes 61448 | tf_op jit(solution)/shard_map/ppermute | solution.py:354
  127.7 1.7 collective-permute-done.20.refs_3_
  129.4 0.6 copy-done.31
  130.0 1.4 shard_map.58.refs_0_
  131.4 1.1 collective-permute-start.21
  132.6 4.1 %collective-permute-done.21.refs_1_ = bf16[4,5,16,128]{3,2,1,0:T(8,128)(2,1)S(1)} collective-permute-done((bf16[4,5,16,128]{3,2,1,0:T(8,128)(2,1)}, bf16[4,5,16,128]{3,2,1,0:T(8,128)(2,1)S(1)}, u32[]{:S(2)}, u32[]{:S(2)}) %collective-permute-start.21) | collective-permute-done | bytes 81952 | tf_op jit(solution)/shard_map/ppermute | solution.py:354
  136.6 2.9 %collective-permute-start.22 = (bf16[4,5,16,128]{3,2,1,0:T(8,128)(2,1)}, bf16[4,5,16,128]{3,2,1,0:T(8,128)(2,1)S(1)}, u32[]{:S(2)}, u32[]{:S(2)}) collective-permute-start(bf16[4,5,16,128]{3,2,1,0:T(8,128)(2,1)} %shard_map.58.refs_0_), channel_id=1, source_target_pairs={{4,0},{5,1},{6,2},{7,3},{8,4},{9,5},{10,6},{11,7},{12,8},{13,9},{1... | collective-permute-start | bytes 245768 | tf_op jit(solution)/shard_map/ppermute | solution.py:354
  139.5 4.8 %collective-permute-done.22.refs_2_ = bf16[4,5,16,128]{3,2,1,0:T(8,128)(2,1)S(1)} collective-permute-done((bf16[4,5,16,128]{3,2,1,0:T(8,128)(2,1)}, bf16[4,5,16,128]{3,2,1,0:T(8,128)(2,1)S(1)}, u32[]{:S(2)}, u32[]{:S(2)}) %collective-permute-start.22) | collective-permute-done | bytes 81952 | tf_op jit(solution)/shard_map/ppermute | solution.py:354
  144.3 3.6 %collective-permute-start.23 = (bf16[4,5,16,128]{3,2,1,0:T(8,128)(2,1)}, bf16[4,5,16,128]{3,2,1,0:T(8,128)(2,1)S(1)}, u32[]{:S(2)}, u32[]{:S(2)}) collective-permute-start(bf16[4,5,16,128]{3,2,1,0:T(8,128)(2,1)} %shard_map.58.refs_0_), channel_id=1, source_target_pairs={{6,0},{7,1},{8,2},{9,3},{10,4},{11,5},{12,6},{13,7},{14,8},{15,9},... | collective-permute-start | bytes 245768 | tf_op jit(solution)/shard_map/ppermute | solution.py:354
  147.9 6.8 %collective-permute-done.23.refs_3_ = bf16[4,5,16,128]{3,2,1,0:T(8,128)(2,1)S(1)} collective-permute-done((bf16[4,5,16,128]{3,2,1,0:T(8,128)(2,1)}, bf16[4,5,16,128]{3,2,1,0:T(8,128)(2,1)S(1)}, u32[]{:S(2)}, u32[]{:S(2)}) %collective-permute-start.23) | collective-permute-done | bytes 81952 | tf_op jit(solution)/shard_map/ppermute | solution.py:354
  154.7 1.9 collective-permute-start.24
  156.6 9.1 %collective-permute-done.24.refs_4_ = bf16[4,5,16,128]{3,2,1,0:T(8,128)(2,1)} collective-permute-done((bf16[4,5,16,128]{3,2,1,0:T(8,128)(2,1)}, bf16[4,5,16,128]{3,2,1,0:T(8,128)(2,1)}, u32[]{:S(2)}, u32[]{:S(2)}) %collective-permute-start.24) | collective-permute-done | bytes 81952 | tf_op jit(solution)/shard_map/ppermute | solution.py:354
  165.7 4.1 %collective-permute-start.25 = (bf16[4,5,16,128]{3,2,1,0:T(8,128)(2,1)}, bf16[4,5,16,128]{3,2,1,0:T(8,128)(2,1)}, u32[]{:S(2)}, u32[]{:S(2)}) collective-permute-start(bf16[4,5,16,128]{3,2,1,0:T(8,128)(2,1)} %shard_map.58.refs_0_), channel_id=1, source_target_pairs={{58,0},{59,1},{60,2},{61,3},{62,4},{63,5},{0,6},{1,7},{2,8},{3,9},... | collective-permute-start | bytes 245768 | tf_op jit(solution)/shard_map/ppermute | solution.py:354
  169.8 3.8 %collective-permute-done.25.refs_5_ = bf16[4,5,16,128]{3,2,1,0:T(8,128)(2,1)} collective-permute-done((bf16[4,5,16,128]{3,2,1,0:T(8,128)(2,1)}, bf16[4,5,16,128]{3,2,1,0:T(8,128)(2,1)}, u32[]{:S(2)}, u32[]{:S(2)}) %collective-permute-start.25) | collective-permute-done | bytes 81952 | tf_op jit(solution)/shard_map/ppermute | solution.py:354
  173.6 0.5 collective-permute-start.26
  174.1 9.6 %collective-permute-done.26.refs_6_ = bf16[4,5,16,128]{3,2,1,0:T(8,128)(2,1)} collective-permute-done((bf16[4,5,16,128]{3,2,1,0:T(8,128)(2,1)}, bf16[4,5,16,128]{3,2,1,0:T(8,128)(2,1)}, u32[]{:S(2)}, u32[]{:S(2)}) %collective-permute-start.26) | collective-permute-done | bytes 81952 | tf_op jit(solution)/shard_map/ppermute | solution.py:354
  183.8 0.0 collective-permute-start.27
  183.8 6.0 %collective-permute-done.27.refs_7_ = bf16[4,5,16,128]{3,2,1,0:T(8,128)(2,1)} collective-permute-done((bf16[4,5,16,128]{3,2,1,0:T(8,128)(2,1)}, bf16[4,5,16,128]{3,2,1,0:T(8,128)(2,1)}, u32[]{:S(2)}, u32[]{:S(2)}) %collective-permute-start.27) | collective-permute-done | bytes 81952 | tf_op jit(solution)/shard_map/ppermute | solution.py:354
  189.7 2.1 shard_map.59.own_ref
  191.8 2.4 %collective-permute-start.31 = (bf16[5,4,4,32,128]{4,3,2,1,0:T(8,128)(2,1)S(1)}, bf16[5,4,4,32,128]{4,3,2,1,0:T(8,128)(2,1)}, u32[]{:S(2)}, u32[]{:S(2)}) collective-permute-start(bf16[5,4,4,32,128]{4,3,2,1,0:T(8,128)(2,1)S(1)} %get-tuple-element.264.refs_2_.own_ref), channel_id=1, source_target_pairs={{0,2},{1,3},{2,4},{3,5},{4,6},{5,7},{6,8},{7,9},{8,10},{9,11},{10,... | collective-permute-start | bytes 1966088 | tf_op jit(solution)/shard_map/ppermute | solution.py:354
  194.2 0.0 collective-permute-done.35.before_ref
  194.3 1.3 collective-permute-start.32
  195.6 0.0 collective-permute-done.36.after_ref
  195.6 5.4 %collective-permute-start.29 = (bf16[5,4,4,32,128]{4,3,2,1,0:T(8,128)(2,1)S(1)}, bf16[5,4,4,32,128]{4,3,2,1,0:T(8,128)(2,1)}, u32[]{:S(2)}, u32[]{:S(2)}) collective-permute-start(bf16[5,4,4,32,128]{4,3,2,1,0:T(8,128)(2,1)S(1)} %get-tuple-element.265.refs_3_.own_ref), channel_id=1, source_target_pairs={{0,2},{1,3},{2,4},{3,5},{4,6},{5,7},{6,8},{7,9},{8,10},{9,11},{10,... | collective-permute-start | bytes 1966088 | tf_op jit(solution)/shard_map/ppermute | solution.py:354
  201.0 1.3 collective-permute-start.30
  202.4 0.9 copy-done.19
  203.3 4.1 %scores.7.score_ref = bf16[4,8,32,384]{3,2,1,0:T(8,128)(2,1)} custom-call(s32[2,128]{1,0:T(2,128)} %reshape.8.bounds_ref, bf16[5,4,4,32,128]{4,3,2,1,0:T(8,128)(2,1)S(1)} %get-tuple-element.262.refs_0_.own_ref, bf16[5,4,4,32,128]{4,3,2,1,0:T(8,128)(2,1)} %copy-done.16, bf16[5,4,4,32,128]{4,3,2,1,0:T(8,128)(2,1)} %copy-done.17), custom_call_target="tpu_custom_call" | custom-call | tf_op jit(solution)/shard_map/scores/pallas_call | solution.py:299
  207.3 4.1 %scores.6.score_ref = bf16[4,8,32,384]{3,2,1,0:T(8,128)(2,1)} custom-call(s32[2,128]{1,0:T(2,128)} %reshape.8.bounds_ref, bf16[5,4,4,32,128]{4,3,2,1,0:T(8,128)(2,1)S(1)} %get-tuple-element.263.refs_1_.own_ref, bf16[5,4,4,32,128]{4,3,2,1,0:T(8,128)(2,1)} %copy-done.18, bf16[5,4,4,32,128]{4,3,2,1,0:T(8,128)(2,1)} %copy-done.19), custom_call_target="tpu_custom_call" | custom-call | tf_op jit(solution)/shard_map/scores/pallas_call | solution.py:299
  211.4 4.1 %scores.5.score_ref = bf16[4,8,32,384]{3,2,1,0:T(8,128)(2,1)} custom-call(s32[2,128]{1,0:T(2,128)} %reshape.8.bounds_ref, bf16[5,4,4,32,128]{4,3,2,1,0:T(8,128)(2,1)S(1)} %get-tuple-element.264.refs_2_.own_ref, bf16[5,4,4,32,128]{4,3,2,1,0:T(8,128)(2,1)} %collective-permute-done.31.before_ref, bf16[5,4,4,32,128]{4,3,2,1,0:T(8,128)(2,1)} %collective-permute-done.32.after_ref), custom_call_target="tpu_custom_call" | custom-call | tf_op jit(solution)/shard_map/scores/pallas_call | solution.py:299
  215.5 4.1 %scores.4.score_ref = bf16[4,8,32,384]{3,2,1,0:T(8,128)(2,1)} custom-call(s32[2,128]{1,0:T(2,128)} %reshape.8.bounds_ref, bf16[5,4,4,32,128]{4,3,2,1,0:T(8,128)(2,1)S(1)} %get-tuple-element.265.refs_3_.own_ref, bf16[5,4,4,32,128]{4,3,2,1,0:T(8,128)(2,1)} %collective-permute-done.29.before_ref, bf16[5,4,4,32,128]{4,3,2,1,0:T(8,128)(2,1)} %collective-permute-done.30.after_ref), custom_call_target="tpu_custom_call" | custom-call | tf_op jit(solution)/shard_map/scores/pallas_call | solution.py:299
  219.7 6.6 %order.2 = bf16[384,1024]{1,0:T(8,128)(2,1)S(1)} custom-call(s32[3]{0:T(128)} %pad_add_fusion.1.place_ref, s32[1,1024]{1,0:T(1,128)S(1)} %bitcast.21, s32[32,1024]{1,0:T(8,128)S(1)} %get-tuple-element.261.rank_ref, bf16[32,5,16,128]{3,2,1,0:T(8,128)(2,1)} %shard_map.59.own_ref, bf16[32,5,16,128]{3,2,1,0:T(8,128)(2,1)} %collective-permute-done.28.other_ref), custom_call_target="tpu_custom_call" | custom-call | tf_op jit(solution)/shard_map/order/pallas_call | solution.py:248
  226.2 0.6 while.10
  226.8 4.4 %correlate.4.refs_0_ = bf16[4,32,32,1024]{3,2,1,0:T(8,128)(2,1)} custom-call(bf16[384,1024]{1,0:T(8,128)(2,1)S(1)} %get-tuple-element.121.table_ref, bf16[4,8,32,384]{3,2,1,0:T(8,128)(2,1)} %scores.7.score_ref), custom_call_target="tpu_custom_call" | custom-call | tf_op jit(solution)/shard_map/correlate/pallas_call | solution.py:319
  231.2 4.3 %correlate.5.refs_0_ = bf16[4,32,32,1024]{3,2,1,0:T(8,128)(2,1)} custom-call(bf16[384,1024]{1,0:T(8,128)(2,1)S(1)} %get-tuple-element.121.table_ref, bf16[4,8,32,384]{3,2,1,0:T(8,128)(2,1)} %scores.6.score_ref, bf16[4,32,32,1024]{3,2,1,0:T(8,128)(2,1)} %correlate.4.refs_0_), custom_call_target="tpu_custom_call", output_to_operand_aliasing={{}: (2, {})} | custom-call | tf_op jit(solution)/shard_map/correlate/pallas_call | solution.py:319
  235.5 4.3 %correlate.6.refs_0_ = bf16[4,32,32,1024]{3,2,1,0:T(8,128)(2,1)} custom-call(bf16[384,1024]{1,0:T(8,128)(2,1)S(1)} %get-tuple-element.121.table_ref, bf16[4,8,32,384]{3,2,1,0:T(8,128)(2,1)} %scores.5.score_ref, bf16[4,32,32,1024]{3,2,1,0:T(8,128)(2,1)} %correlate.5.refs_0_), custom_call_target="tpu_custom_call", output_to_operand_aliasing={{}: (2, {})} | custom-call | tf_op jit(solution)/shard_map/correlate/pallas_call | solution.py:319
  239.8 4.3 %correlate.7 = bf16[4,32,32,1024]{3,2,1,0:T(8,128)(2,1)} custom-call(bf16[384,1024]{1,0:T(8,128)(2,1)S(1)} %get-tuple-element.121.table_ref, bf16[4,8,32,384]{3,2,1,0:T(8,128)(2,1)} %scores.4.score_ref, bf16[4,32,32,1024]{3,2,1,0:T(8,128)(2,1)} %correlate.6.refs_0_), custom_call_target="tpu_custom_call", output_to_operand_aliasing={{}: (2, {})} | custom-call | tf_op jit(solution)/shard_map/correlate/pallas_call | solution.py:319
  (41 shorter events, 0.1 us)
Async XLA Ops:
  0.0 20.3 %copy-start.15 = (s32[1024]{0:T(1024)S(1)}, s32[1024]{0:T(1024)}, u32[]{:S(2)}) copy-start(s32[1024]{0:T(1024)} %param.9) | copy-start | bytes 12292
  1.2 3.7 %collective-permute-start.14 = (f32[4,4,32,300]{3,2,1,0:T(8,128)S(1)}, f32[4,4,32,300]{3,2,1,0:T(8,128)S(1)}, u32[]{:S(2)}, u32[]{:S(2)}) collective-permute-start(f32[4,4,32,300]{3,2,1,0:T(8,128)S(1)} %dynamic-slice_bitcast_fusion), channel_id=1, source_target_pairs={{1,0},{0,1},{3,2},{2,3},{5,4},{4,5},{7,6},{6,7},{9,8},{8,9},{11,10... | collective-permute-start | bytes 1843208 | tf_op jit(solution)/shard_map/ppermute | solution.py:354
  4.9 0.9 copy-start.14
  20.3 182.1 %copy-start = (bf16[5,4,4,32,128]{4,3,2,1,0:T(8,128)(2,1)}, bf16[5,4,4,32,128]{4,3,2,1,0:T(8,128)(2,1)S(1)}, u32[]{:S(2)}) copy-start(bf16[5,4,4,32,128]{4,3,2,1,0:T(8,128)(2,1)S(1)} %get-tuple-element.266.refs_4_) | copy-start | bytes 1966084
  20.3 182.1 %copy-start.1 = (bf16[5,4,4,32,128]{4,3,2,1,0:T(8,128)(2,1)}, bf16[5,4,4,32,128]{4,3,2,1,0:T(8,128)(2,1)S(1)}, u32[]{:S(2)}) copy-start(bf16[5,4,4,32,128]{4,3,2,1,0:T(8,128)(2,1)S(1)} %get-tuple-element.267.refs_5_) | copy-start | bytes 1966084
  20.3 182.1 %copy-start.2 = (bf16[5,4,4,32,128]{4,3,2,1,0:T(8,128)(2,1)}, bf16[5,4,4,32,128]{4,3,2,1,0:T(8,128)(2,1)S(1)}, u32[]{:S(2)}) copy-start(bf16[5,4,4,32,128]{4,3,2,1,0:T(8,128)(2,1)S(1)} %get-tuple-element.268.refs_6_) | copy-start | bytes 1966084
  20.3 182.1 %copy-start.3 = (bf16[5,4,4,32,128]{4,3,2,1,0:T(8,128)(2,1)}, bf16[5,4,4,32,128]{4,3,2,1,0:T(8,128)(2,1)S(1)}, u32[]{:S(2)}) copy-start(bf16[5,4,4,32,128]{4,3,2,1,0:T(8,128)(2,1)S(1)} %get-tuple-element.269.refs_7_) | copy-start | bytes 1966084
  25.0 1.7 collective-permute-start.15
  26.7 0.7 copy-start.23
  29.0 16.1 %collective-permute-start.16 = (f32[32,384]{1,0:T(8,128)}, f32[32,384]{1,0:T(8,128)S(1)}, u32[]{:S(2)}, u32[]{:S(2)}) collective-permute-start(f32[32,384]{1,0:T(8,128)} %get-tuple-element.118), channel_id=1, source_target_pairs={{0,2},{1,3},{2,4},{3,5},{4,6},{5,7},{6,8},{7,9},{8,10},{9,11},{10,... | collective-permute-start | bytes 147464 | tf_op jit(solution)/shard_map/ppermute | solution.py:354
  33.0 13.4 %collective-permute-start.17 = (f32[32,384]{1,0:T(8,128)}, f32[32,384]{1,0:T(8,128)S(1)}, u32[]{:S(2)}, u32[]{:S(2)}) collective-permute-start(f32[32,384]{1,0:T(8,128)} %get-tuple-element.119), channel_id=1, source_target_pairs={{2,0},{3,1},{4,2},{5,3},{6,4},{7,5},{8,6},{9,7},{10,8},{11,9},{12,... | collective-permute-start | bytes 147464 | tf_op jit(solution)/shard_map/ppermute | solution.py:354
  34.3 159.9 %collective-permute-start.35 = (bf16[5,4,4,32,128]{4,3,2,1,0:T(8,128)(2,1)S(1)}, bf16[5,4,4,32,128]{4,3,2,1,0:T(8,128)(2,1)S(1)}, u32[]{:S(2)}, u32[]{:S(2)}) collective-permute-start(bf16[5,4,4,32,128]{4,3,2,1,0:T(8,128)(2,1)S(1)} %get-tuple-element.262.refs_0_.own_ref), channel_id=1, source_target_pairs={{0,2},{1,3},{2,4},{3,5},{4,6},{5,7},{6,8},{7,9},{8,10},{9,11},{10,... | collective-permute-start | bytes 1966088 | tf_op jit(solution)/shard_map/ppermute | solution.py:354
  39.1 156.5 %collective-permute-start.36 = (bf16[5,4,4,32,128]{4,3,2,1,0:T(8,128)(2,1)S(1)}, bf16[5,4,4,32,128]{4,3,2,1,0:T(8,128)(2,1)S(1)}, u32[]{:S(2)}, u32[]{:S(2)}) collective-permute-start(bf16[5,4,4,32,128]{4,3,2,1,0:T(8,128)(2,1)S(1)} %get-tuple-element.262.refs_0_.own_ref), channel_id=1, source_target_pairs={{2,0},{3,1},{4,2},{5,3},{6,4},{7,5},{8,6},{9,7},{10,8},{11,9},{12,... | collective-permute-start | bytes 1966088 | tf_op jit(solution)/shard_map/ppermute | solution.py:354
  40.4 160.6 %collective-permute-start.33 = (bf16[5,4,4,32,128]{4,3,2,1,0:T(8,128)(2,1)S(1)}, bf16[5,4,4,32,128]{4,3,2,1,0:T(8,128)(2,1)S(1)}, u32[]{:S(2)}, u32[]{:S(2)}) collective-permute-start(bf16[5,4,4,32,128]{4,3,2,1,0:T(8,128)(2,1)S(1)} %get-tuple-element.263.refs_1_.own_ref), channel_id=1, source_target_pairs={{0,2},{1,3},{2,4},{3,5},{4,6},{5,7},{6,8},{7,9},{8,10},{9,11},{10,... | collective-permute-start | bytes 1966088 | tf_op jit(solution)/shard_map/ppermute | solution.py:354
  45.1 1.4 copy-start.27
  45.1 157.2 %collective-permute-start.34 = (bf16[5,4,4,32,128]{4,3,2,1,0:T(8,128)(2,1)S(1)}, bf16[5,4,4,32,128]{4,3,2,1,0:T(8,128)(2,1)S(1)}, u32[]{:S(2)}, u32[]{:S(2)}) collective-permute-start(bf16[5,4,4,32,128]{4,3,2,1,0:T(8,128)(2,1)S(1)} %get-tuple-element.263.refs_1_.own_ref), channel_id=1, source_target_pairs={{2,0},{3,1},{4,2},{5,3},{6,4},{7,5},{8,6},{9,7},{10,8},{11,9},{12,... | collective-permute-start | bytes 1966088 | tf_op jit(solution)/shard_map/ppermute | solution.py:354
  46.5 0.6 copy-start.28
  48.7 39.0 %collective-permute-start.18 = (bf16[5,16,128]{2,1,0:T(8,128)(2,1)}, bf16[5,16,128]{2,1,0:T(8,128)(2,1)S(1)}, u32[]{:S(2)}, u32[]{:S(2)}) collective-permute-start(bf16[5,16,128]{2,1,0:T(8,128)(2,1)} %shard_map.57.refs_0_), channel_id=1, source_target_pairs={{16,0},{17,1},{18,2},{19,3},{20,4},{21,5},{22,6},{23,7},{24,8},{25... | collective-permute-start | bytes 61448 | tf_op jit(solution)/shard_map/ppermute | solution.py:354
  87.7 41.7 %copy-start.29 = (bf16[5,16,128]{2,1,0:T(8,128)(2,1)}, bf16[5,16,128]{2,1,0:T(8,128)(2,1)S(1)}, u32[]{:S(2)}) copy-start(bf16[5,16,128]{2,1,0:T(8,128)(2,1)S(1)} %collective-permute-done.18.refs_1_) | copy-start | bytes 61444
  87.7 23.3 %collective-permute-start.19 = (bf16[5,16,128]{2,1,0:T(8,128)(2,1)}, bf16[5,16,128]{2,1,0:T(8,128)(2,1)S(1)}, u32[]{:S(2)}, u32[]{:S(2)}) collective-permute-start(bf16[5,16,128]{2,1,0:T(8,128)(2,1)} %shard_map.57.refs_0_), channel_id=1, source_target_pairs={{32,0},{33,1},{34,2},{35,3},{36,4},{37,5},{38,6},{39,7},{40,8},{41... | collective-permute-start | bytes 61448 | tf_op jit(solution)/shard_map/ppermute | solution.py:354
  111.0 18.4 %copy-start.30 = (bf16[5,16,128]{2,1,0:T(8,128)(2,1)}, bf16[5,16,128]{2,1,0:T(8,128)(2,1)S(1)}, u32[]{:S(2)}) copy-start(bf16[5,16,128]{2,1,0:T(8,128)(2,1)S(1)} %collective-permute-done.19.refs_2_) | copy-start | bytes 61444
  111.0 18.4 %collective-permute-start.20 = (bf16[5,16,128]{2,1,0:T(8,128)(2,1)}, bf16[5,16,128]{2,1,0:T(8,128)(2,1)S(1)}, u32[]{:S(2)}, u32[]{:S(2)}) collective-permute-start(bf16[5,16,128]{2,1,0:T(8,128)(2,1)} %shard_map.57.refs_0_), channel_id=1, source_target_pairs={{48,0},{49,1},{50,2},{51,3},{52,4},{53,5},{54,6},{55,7},{56,8},{57... | collective-permute-start | bytes 61448 | tf_op jit(solution)/shard_map/ppermute | solution.py:354
  129.4 0.6 copy-start.31
  131.4 5.2 %collective-permute-start.21 = (bf16[4,5,16,128]{3,2,1,0:T(8,128)(2,1)}, bf16[4,5,16,128]{3,2,1,0:T(8,128)(2,1)S(1)}, u32[]{:S(2)}, u32[]{:S(2)}) collective-permute-start(bf16[4,5,16,128]{3,2,1,0:T(8,128)(2,1)} %shard_map.58.refs_0_), channel_id=1, source_target_pairs={{2,0},{3,1},{4,2},{5,3},{6,4},{7,5},{8,6},{9,7},{10,8},{11,9},{12,... | collective-permute-start | bytes 245768 | tf_op jit(solution)/shard_map/ppermute | solution.py:354
  136.6 53.1 %copy-start.24 = (bf16[4,5,16,128]{3,2,1,0:T(8,128)(2,1)}, bf16[4,5,16,128]{3,2,1,0:T(8,128)(2,1)S(1)}, u32[]{:S(2)}) copy-start(bf16[4,5,16,128]{3,2,1,0:T(8,128)(2,1)S(1)} %collective-permute-done.21.refs_1_) | copy-start | bytes 245764
  136.6 7.7 %collective-permute-start.22 = (bf16[4,5,16,128]{3,2,1,0:T(8,128)(2,1)}, bf16[4,5,16,128]{3,2,1,0:T(8,128)(2,1)S(1)}, u32[]{:S(2)}, u32[]{:S(2)}) collective-permute-start(bf16[4,5,16,128]{3,2,1,0:T(8,128)(2,1)} %shard_map.58.refs_0_), channel_id=1, source_target_pairs={{4,0},{5,1},{6,2},{7,3},{8,4},{9,5},{10,6},{11,7},{12,8},{13,9},{1... | collective-permute-start | bytes 245768 | tf_op jit(solution)/shard_map/ppermute | solution.py:354
  144.3 45.4 %copy-start.25 = (bf16[4,5,16,128]{3,2,1,0:T(8,128)(2,1)}, bf16[4,5,16,128]{3,2,1,0:T(8,128)(2,1)S(1)}, u32[]{:S(2)}) copy-start(bf16[4,5,16,128]{3,2,1,0:T(8,128)(2,1)S(1)} %collective-permute-done.22.refs_2_) | copy-start | bytes 245764
  144.3 10.4 %collective-permute-start.23 = (bf16[4,5,16,128]{3,2,1,0:T(8,128)(2,1)}, bf16[4,5,16,128]{3,2,1,0:T(8,128)(2,1)S(1)}, u32[]{:S(2)}, u32[]{:S(2)}) collective-permute-start(bf16[4,5,16,128]{3,2,1,0:T(8,128)(2,1)} %shard_map.58.refs_0_), channel_id=1, source_target_pairs={{6,0},{7,1},{8,2},{9,3},{10,4},{11,5},{12,6},{13,7},{14,8},{15,9},... | collective-permute-start | bytes 245768 | tf_op jit(solution)/shard_map/ppermute | solution.py:354
  154.7 35.0 %copy-start.26 = (bf16[4,5,16,128]{3,2,1,0:T(8,128)(2,1)}, bf16[4,5,16,128]{3,2,1,0:T(8,128)(2,1)S(1)}, u32[]{:S(2)}) copy-start(bf16[4,5,16,128]{3,2,1,0:T(8,128)(2,1)S(1)} %collective-permute-done.23.refs_3_) | copy-start | bytes 245764
  154.7 11.0 %collective-permute-start.24 = (bf16[4,5,16,128]{3,2,1,0:T(8,128)(2,1)}, bf16[4,5,16,128]{3,2,1,0:T(8,128)(2,1)}, u32[]{:S(2)}, u32[]{:S(2)}) collective-permute-start(bf16[4,5,16,128]{3,2,1,0:T(8,128)(2,1)} %shard_map.58.refs_0_), channel_id=1, source_target_pairs={{8,0},{9,1},{10,2},{11,3},{12,4},{13,5},{14,6},{15,7},{16,8},{17,9... | collective-permute-start | bytes 245768 | tf_op jit(solution)/shard_map/ppermute | solution.py:354
  165.7 7.9 %collective-permute-start.25 = (bf16[4,5,16,128]{3,2,1,0:T(8,128)(2,1)}, bf16[4,5,16,128]{3,2,1,0:T(8,128)(2,1)}, u32[]{:S(2)}, u32[]{:S(2)}) collective-permute-start(bf16[4,5,16,128]{3,2,1,0:T(8,128)(2,1)} %shard_map.58.refs_0_), channel_id=1, source_target_pairs={{58,0},{59,1},{60,2},{61,3},{62,4},{63,5},{0,6},{1,7},{2,8},{3,9},... | collective-permute-start | bytes 245768 | tf_op jit(solution)/shard_map/ppermute | solution.py:354
  173.6 10.2 %collective-permute-start.26 = (bf16[4,5,16,128]{3,2,1,0:T(8,128)(2,1)}, bf16[4,5,16,128]{3,2,1,0:T(8,128)(2,1)}, u32[]{:S(2)}, u32[]{:S(2)}) collective-permute-start(bf16[4,5,16,128]{3,2,1,0:T(8,128)(2,1)} %shard_map.58.refs_0_), channel_id=1, source_target_pairs={{60,0},{61,1},{62,2},{63,3},{0,4},{1,5},{2,6},{3,7},{4,8},{5,9},{6... | collective-permute-start | bytes 245768 | tf_op jit(solution)/shard_map/ppermute | solution.py:354
  183.8 6.0 %collective-permute-start.27 = (bf16[4,5,16,128]{3,2,1,0:T(8,128)(2,1)}, bf16[4,5,16,128]{3,2,1,0:T(8,128)(2,1)}, u32[]{:S(2)}, u32[]{:S(2)}) collective-permute-start(bf16[4,5,16,128]{3,2,1,0:T(8,128)(2,1)} %shard_map.58.refs_0_), channel_id=1, source_target_pairs={{62,0},{63,1},{0,2},{1,3},{2,4},{3,5},{4,6},{5,7},{6,8},{7,9},{8,1... | collective-permute-start | bytes 245768 | tf_op jit(solution)/shard_map/ppermute | solution.py:354
  191.8 19.6 %collective-permute-start.31 = (bf16[5,4,4,32,128]{4,3,2,1,0:T(8,128)(2,1)S(1)}, bf16[5,4,4,32,128]{4,3,2,1,0:T(8,128)(2,1)}, u32[]{:S(2)}, u32[]{:S(2)}) collective-permute-start(bf16[5,4,4,32,128]{4,3,2,1,0:T(8,128)(2,1)S(1)} %get-tuple-element.264.refs_2_.own_ref), channel_id=1, source_target_pairs={{0,2},{1,3},{2,4},{3,5},{4,6},{5,7},{6,8},{7,9},{8,10},{9,11},{10,... | collective-permute-start | bytes 1966088 | tf_op jit(solution)/shard_map/ppermute | solution.py:354
  194.2 9.0 %copy-start.16 = (bf16[5,4,4,32,128]{4,3,2,1,0:T(8,128)(2,1)}, bf16[5,4,4,32,128]{4,3,2,1,0:T(8,128)(2,1)S(1)}, u32[]{:S(2)}) copy-start(bf16[5,4,4,32,128]{4,3,2,1,0:T(8,128)(2,1)S(1)} %collective-permute-done.35.before_ref) | copy-start | bytes 1966084
  194.3 17.2 %collective-permute-start.32 = (bf16[5,4,4,32,128]{4,3,2,1,0:T(8,128)(2,1)S(1)}, bf16[5,4,4,32,128]{4,3,2,1,0:T(8,128)(2,1)}, u32[]{:S(2)}, u32[]{:S(2)}) collective-permute-start(bf16[5,4,4,32,128]{4,3,2,1,0:T(8,128)(2,1)S(1)} %get-tuple-element.264.refs_2_.own_ref), channel_id=1, source_target_pairs={{2,0},{3,1},{4,2},{5,3},{6,4},{7,5},{8,6},{9,7},{10,8},{11,9},{12,... | collective-permute-start | bytes 1966088 | tf_op jit(solution)/shard_map/ppermute | solution.py:354
  195.6 6.8 %copy-start.17 = (bf16[5,4,4,32,128]{4,3,2,1,0:T(8,128)(2,1)}, bf16[5,4,4,32,128]{4,3,2,1,0:T(8,128)(2,1)S(1)}, u32[]{:S(2)}) copy-start(bf16[5,4,4,32,128]{4,3,2,1,0:T(8,128)(2,1)S(1)} %collective-permute-done.36.after_ref) | copy-start | bytes 1966084
  195.6 20.0 %collective-permute-start.29 = (bf16[5,4,4,32,128]{4,3,2,1,0:T(8,128)(2,1)S(1)}, bf16[5,4,4,32,128]{4,3,2,1,0:T(8,128)(2,1)}, u32[]{:S(2)}, u32[]{:S(2)}) collective-permute-start(bf16[5,4,4,32,128]{4,3,2,1,0:T(8,128)(2,1)S(1)} %get-tuple-element.265.refs_3_.own_ref), channel_id=1, source_target_pairs={{0,2},{1,3},{2,4},{3,5},{4,6},{5,7},{6,8},{7,9},{8,10},{9,11},{10,... | collective-permute-start | bytes 1966088 | tf_op jit(solution)/shard_map/ppermute | solution.py:354
  201.0 1.4 copy-start.18
  201.0 14.5 %collective-permute-start.30 = (bf16[5,4,4,32,128]{4,3,2,1,0:T(8,128)(2,1)S(1)}, bf16[5,4,4,32,128]{4,3,2,1,0:T(8,128)(2,1)}, u32[]{:S(2)}, u32[]{:S(2)}) collective-permute-start(bf16[5,4,4,32,128]{4,3,2,1,0:T(8,128)(2,1)S(1)} %get-tuple-element.265.refs_3_.own_ref), channel_id=1, source_target_pairs={{2,0},{3,1},{4,2},{5,3},{6,4},{7,5},{8,6},{9,7},{10,8},{11,9},{12,... | collective-permute-start | bytes 1966088 | tf_op jit(solution)/shard_map/ppermute | solution.py:354
  202.4 0.9 copy-start.19
  203.3 16.4 %collective-permute-start.28 = (bf16[32,5,16,128]{3,2,1,0:T(8,128)(2,1)}, bf16[32,5,16,128]{3,2,1,0:T(8,128)(2,1)}, u32[]{:S(2)}, u32[]{:S(2)}) collective-permute-start(bf16[32,5,16,128]{3,2,1,0:T(8,128)(2,1)} %shard_map.59.own_ref), channel_id=1, source_target_pairs={{1,0},{0,1},{3,2},{2,3},{5,4},{4,5},{7,6},{6,7},{9,8},{8,9},{11,10... | collective-permute-start | bytes 1966088 | tf_op jit(solution)/shard_map/ppermute | solution.py:354

commit v3 on v2

--- a/solution.py
+++ b/solution.py
@@ -51,12 +51,8 @@
         th, tl = taps_high[:size, :size], taps_low[:size, :size]
         return (dot(th, head) + dot(th, rest) + dot(tl, head)).reshape(count, cells_z, lanes)
 
-    def two_groups(step, _):
-        for k in range(2):
-            at = (2 * step + k) * group
-            wide[pl.ds(REACH + at, group)] = along_z(bold_ref[0, pl.ds(at, group)], group)
-
-    lax.fori_loop(0, rows // group // 2, two_groups, None)
+    for at in range(0, rows, group):
+        wide[REACH + at : REACH + at + group] = along_z(bold_ref[0, at : at + group], group)
     edge = along_z(edge_ref[0], REACH)
     wide[:REACH] = jnp.where(side == 1, edge, 0.0)
     wide[REACH + rows :] = jnp.where(side == 1, 0.0, edge)
@@ -114,16 +110,21 @@
     return outs[:NCHUNK], outs[NCHUNK:]
 
 
-def rank_kernel(row_ref, out_ref, turns_ref, *, column):
-    seeds, chips = row_ref.shape[1], out_ref.shape[0]
-    seed = row_ref[...]
+def rank_kernel(row_ref, block_ref, out_ref, turns_ref, *, column):
+    seeds, chips, count = row_ref.shape[1], out_ref.shape[0], block_ref.shape[1]
+    step = pl.program_id(0)
     chip = lax.broadcasted_iota(jnp.int32, (chips, 1), 0) * column
-    here = jnp.where((seed >= chip) & (seed < chip + column), 1.0, 0.0)
-    earlier = lax.broadcasted_iota(jnp.int32, (seeds, seeds), 0) < lax.broadcasted_iota(jnp.int32, (seeds, seeds), 1)
-    before = dot(here.astype(BF), jnp.where(earlier, 1.0, 0.0).astype(BF))
-    rank = jnp.sum(here * before, axis=0, keepdims=True)
+
+    def here(seed):
+        return jnp.where((seed >= chip) & (seed < chip + column), 1.0, 0.0)
+
+    down, across = (lax.broadcasted_iota(jnp.int32, (seeds, count), axis) for axis in (0, 1))
+    earlier = jnp.where(down < across + step * count, 1.0, 0.0).astype(BF)
+    before = dot(here(row_ref[...]).astype(BF), earlier)
+    rank = jnp.sum(here(block_ref[...]) * before, axis=0, keepdims=True)
     out_ref[...] = jnp.broadcast_to(rank.astype(jnp.int32), out_ref.shape)
-    turns_ref[0] = (jnp.max(rank).astype(jnp.int32) + LIST) // LIST
+    turns = (jnp.max(rank).astype(jnp.int32) + LIST) // LIST
+    turns_ref[0] = jnp.maximum(turns, jnp.where(step == 0, 0, turns_ref[0]))
 
 
 def part_kernel(place_ref, row_ref, rank_ref, *refs, cells, column, strip):
@@ -211,7 +212,7 @@
     return call(join_kernel, jax.ShapeDtypeStruct(shape, pieces[0].dtype), *pieces)
 
 
-def order_kernel(place_ref, row_ref, rank_ref, own_ref, other_ref, out_ref, *, column):
+def order_kernel(place_ref, row_ref, rank_ref, own_ref, other_ref, out_ref, *, column, both_ways):
     side, turn = place_ref[1], place_ref[2]
     half = HALF // 2
     count = own_ref.shape[0] * half
@@ -224,7 +225,8 @@
     ahead = jnp.where(ahead < 0, ahead + size, ahead)
     far = ahead // fourth
     low = ahead - far * fourth
-    far = jnp.where(2 * low > fourth, far + 1, far)
+    if both_ways:
+        far = jnp.where(2 * low > fourth, far + 1, far)
     block = low * 4 + jnp.where(far >= 4, far - 4, far)
     spot = part * count + block * half + rank - quarter * half
     spot = jnp.where((rank >= 0) & (rank < LIST), spot, -1)
@@ -243,10 +245,10 @@
     out_ref[2 * LANES :] = jnp.concatenate([last, jnp.zeros_like(last)], axis=0).astype(BF)
 
 
-def in_order(place, row, ranks, own, other, column):
-    seeds, block = row.shape[1], 128
+def in_order(place, row, ranks, own, other, column, both_ways):
+    seeds, block = row.shape[1], 256
     return pl.pallas_call(
-        functools.partial(order_kernel, column=column),
+        functools.partial(order_kernel, column=column, both_ways=both_ways),
         grid=(seeds // block,),
         in_specs=[
             pl.BlockSpec(memory_space=pltpu.SMEM),
@@ -261,7 +263,8 @@
     )(place, row, ranks, own, other)
 
 
-def scores_kernel(bounds_ref, own_ref, before_ref, after_ref, out_ref, *, frames, first):
+def scores_kernel(bounds_ref, own_ref, before_ref, after_ref, *refs, frames, first):
+    out_ref = refs[-1]
     cells_x, cells_z = own_ref.shape[1], own_ref.shape[3]
     pair = first + pl.program_id(0)
     near = lax.broadcasted_iota(jnp.int32, (1, LANES), 1) < LANES // 2
@@ -293,42 +296,43 @@
                 out_ref[x, odd, :, k * LANES : (k + 1) * LANES] = (piece * scale).astype(BF)
 
 
-def scores(bounds, own, before, after, frames, index):
+def scores(bounds, own, before, after, out, frames, index):
     _, cells_x, pairs, cells_z, _ = own.shape
+    first = sum(PAIRS[:index])
     spec = pl.BlockSpec((5, cells_x, 1, cells_z, LANES), lambda p: (0, 0, p, 0, 0))
+    more = [] if out is None else [out]
     return pl.pallas_call(
-        functools.partial(scores_kernel, frames=frames, first=sum(PAIRS[:index])),
+        functools.partial(scores_kernel, frames=frames, first=first),
         grid=(pairs,),
-        in_specs=[pl.BlockSpec(memory_space=pltpu.SMEM), spec, spec, spec],
-        out_specs=pl.BlockSpec((cells_x, 2, cells_z, 3 * LANES), lambda p: (0, p, 0, 0)),
-        out_shape=jax.ShapeDtypeStruct((cells_x, 2 * pairs, cells_z, 3 * LANES), BF),
+        in_specs=[pl.BlockSpec(memory_space=pltpu.SMEM), spec, spec, spec]
+        + [pl.BlockSpec(memory_space=pl.ANY)] * len(more),
+        out_specs=pl.BlockSpec((cells_x, 2, cells_z, 3 * LANES), lambda p: (0, first + p, 0, 0)),
+        out_shape=jax.ShapeDtypeStruct((cells_x, 2 * sum(PAIRS), cells_z, 3 * LANES), BF),
+        input_output_aliases={4: 0} if more else {},
         name="scores",
-    )(bounds, own, before, after)
-
-
-def correlate_kernel(table_ref, score_ref, *refs, frames):
-    out_ref = refs[-1]
+    )(bounds, own, before, after, *more)
+
+
+def correlate_kernel(table_ref, score_ref, out_ref, *, frames):
     corr = dot(score_ref[...].reshape(-1, table_ref.shape[0]), table_ref[...]) * (1.0 / frames)
     out_ref[...] = corr.astype(BF).reshape(out_ref.shape)
 
 
-def correlate(table, score, out, shape, frames, index):
+def correlate(table, score, frames):
     cells_x, rows, cells_z, lanes = score.shape
-    first = sum(PAIRS[:index])
-    more = [] if out is None else [out]
+    block, seeds = 4, table.shape[1]
     return pl.pallas_call(
         functools.partial(correlate_kernel, frames=frames),
-        grid=(rows // 2,),
+        grid=(rows // block,),
         in_specs=[
             pl.BlockSpec(table.shape, lambda p: (0, 0)),
-            pl.BlockSpec((cells_x, 2, cells_z, lanes), lambda p: (0, p, 0, 0)),
-        ]
-        + [pl.BlockSpec(memory_space=pl.ANY)] * len(more),
-        out_specs=pl.BlockSpec((cells_x, 2, cells_z, shape[-1]), lambda p: (0, first + p, 0, 0)),
-        out_shape=jax.ShapeDtypeStruct(shape, BF),
-        input_output_aliases={2: 0} if more else {},
+            pl.BlockSpec((cells_x, block, cells_z, lanes), lambda p: (0, p, 0, 0)),
+        ],
+        out_specs=pl.BlockSpec((cells_x, block, cells_z, seeds), lambda p: (0, p, 0, 0)),
+        out_shape=jax.ShapeDtypeStruct((cells_x, rows, cells_z, seeds), BF),
+        compiler_params=pltpu.CompilerParams(vmem_limit_bytes=VMEM),
         name="correlate",
-    )(table, score, *more)
+    )(table, score)
 
 
 def call(kernel, out, *args, smem=0):
@@ -374,17 +378,18 @@
     row = seed_index.reshape(1, seeds)
     ranks, turns = pl.pallas_call(
         functools.partial(rank_kernel, column=column),
-        in_specs=[pl.BlockSpec(memory_space=pltpu.VMEM)],
-        out_specs=[pl.BlockSpec(memory_space=pltpu.VMEM), pl.BlockSpec(memory_space=pltpu.SMEM)],
+        grid=(seeds // 256,),
+        in_specs=[pl.BlockSpec((1, seeds), lambda i: (0, 0)), pl.BlockSpec((1, 256), lambda i: (0, i))],
+        out_specs=[pl.BlockSpec((size, 256), lambda i: (0, i)), pl.BlockSpec(memory_space=pltpu.SMEM)],
         out_shape=[jax.ShapeDtypeStruct((size, seeds), jnp.int32), jax.ShapeDtypeStruct((1,), jnp.int32)],
         name="rank",
-    )(row)
+    )(row, row)
 
     fourth = size // 4
     far_steps = [k * fourth for k in range(1, 4)]
     near_steps = [k if 2 * k <= fourth else k - fourth for k in range(1, fourth)]
 
-    def table_of(turn):
+    def table_of(turn, doubling):
         place = jnp.stack([brick, side, turn]).astype(jnp.int32)
         own, other = call(
             functools.partial(part_kernel, cells=(cells_x, cells_y, cells_z), column=column, strip=strip),
@@ -409,22 +414,26 @@
         )
         far = [mine] + [shift(mine, step, wrap=True) for step in far_steps]
         some = join(far)
-        near = [some] + [shift(some, step, wrap=True) for step in near_steps]
-        every = join(near)
+        if doubling:
+            every, step = some, 1
+            while step < fourth:
+                every = join([every, shift(every, step, wrap=True)])
+                step *= 2
+        else:
+            near = [some] + [shift(some, step, wrap=True) for step in near_steps]
+            every = join(near)
         other = shift(every, 0, flip=True)
-        return in_order(place, row, ranks, every, other, column)
-
-    table = table_of(jnp.int32(0))
+        return in_order(place, row, ranks, every, other, column, not doubling)
+
+    table = table_of(jnp.int32(0), False)
     _, table = lax.while_loop(
-        lambda s: s[0] < turns[0], lambda s: (s[0] + 1, s[1] + table_of(s[0])), (jnp.int32(1), table)
+        lambda s: s[0] < turns[0], lambda s: (s[0] + 1, s[1] + table_of(s[0], True)), (jnp.int32(1), table)
     )
 
-    shape = (cells_x, cells_y, cells_z, seeds)
-    out = None
+    score = None
     for index in range(NCHUNK):
-        score = scores(bounds, chunks[index], *halos[index], frames, index)
-        out = correlate(table, score, out, shape, frames, index)
-    return out
+        score = scores(bounds, chunks[index], *halos[index], score, frames, index)
+    return correlate(table, score, frames)
 
 
 def solution(mesh):

time: 247 us -> 237 us (0.960)
  the two profiles are of different devices: /device:TPU:44 before, /device:TPU:37 now
where the time goes in v3:
time: 237 us; the launch traced here: 236 us
  starting transfers between devices  129 us (54%)
  Pallas kernels  57.3 us (24%)
  waiting for transfers between devices  41.6 us (18%)
  local copies, waits for them, and re-layouts  6.13 us (3%)
    ppermute x23, starting transfers between devices, shift(): return lax.ppermute(value, ('gx', 'gy'), pairs)  129 us
    ppermute x23, waiting for transfers between devices, shift(): return lax.ppermute(value, ('gx', 'gy'), pairs)  41.6 us
    pallas_call x4, Pallas kernels, scores(): pl.pallas_call(functools.partial(scores_kernel, frames=frames, first=firs...  16.5 us
    pallas_call x1, Pallas kernels, in_plane(): pl.pallas_call(functools.partial(in_plane_kernel, frames=frames), grid=(c...  12.3 us
    pallas_call x5, Pallas kernels, call(): pl.pallas_call(kernel, in_specs=in_specs, out_specs=[pl.BlockSpec(memory_...  11.4 us
    pallas_call x1, Pallas kernels, correlate(): pl.pallas_call(functools.partial(correlate_kernel, frames=frames), grid=(...  9.76 us
  transfers between devices with their start and end apart: 23, of which 11 were waited for; matrix products, arithmetic and copies ran while one was open for 1% of the time, Pallas kernels for 10%

profile of v3, /device:TPU:37, one launch (start us, length us, event | category | flops | bytes accessed | tf_op | source)
XLA Modules:
  0.0 236.2 jit_solution(12730887249701038871)
XLA Ops:
  0.0 1.2 dynamic-slice_bitcast_fusion
  1.2 20.5 %collective-permute-start.10 = (f32[4,4,32,300]{3,2,1,0:T(8,128)S(1)}, f32[4,4,32,300]{3,2,1,0:T(8,128)S(1)}, u32[]{:S(2)}, u32[]{:S(2)}) collective-permute-start(f32[4,4,32,300]{3,2,1,0:T(8,128)S(1)} %dynamic-slice_bitcast_fusion), channel_id=1, source_target_pairs={{1,0},{0,1},{3,2},{2,3},{5,4},{4,5},{7,6},{6,7},{9,8},{8,9},{11,10... | collective-permute-start | bytes 1843208 | tf_op jit(solution)/shard_map/ppermute | solution.py:358
  21.7 0.7 copy.9
  22.4 0.6 reshape.8.bounds_ref
  23.0 3.0 %rank.1 = (s32[32,1024]{1,0:T(8,128)S(1)}, s32[1]{0:T(128)}) custom-call(s32[1,1024]{1,0:T(1,128)} %bitcast.19, s32[1,1024]{1,0:T(1,128)} %bitcast.20), custom_call_target="tpu_custom_call" | custom-call | tf_op jit(solution)/shard_map/rank/pallas_call | solution.py:379
  26.1 0.7 pad_add_fusion.1.place_ref
  26.7 0.9 copy-done.11
  27.6 12.3 %in_plane.1 = (bf16[5,4,4,32,128]{4,3,2,1,0:T(8,128)(2,1)S(1)}, bf16[5,4,4,32,128]{4,3,2,1,0:T(8,128)(2,1)S(1)}, bf16[5,4,4,32,128]{4,3,2,1,0:T(8,128)(2,1)S(1)}...) custom-call(s32[1]{0:T(128)} %bitcast.5.side_ref, ...), custom_call_target="tpu_custom_call" | custom-call | tf_op jit(solution)/shard_map/in_plane/pallas_call | solution.py:94
  40.0 4.7 %shard_map.55 = (f32[96,384]{1,0:T(8,128)}, f32[96,384]{1,0:T(8,128)}) custom-call(s32[3]{0:T(128)} %pad_add_fusion.1.place_ref, s32[1,1024]{1,0:T(1,128)S(1)} %bitcast.21, s32[32,1024]{1,0:T(8,128)S(1)} %get-tuple-element.261.rank_ref, bf16[5,4,4,32,128]{4,3,2,1,0:T(8,128)(2,1)S(1)} %get-tuple-element.262.refs_0_.own_ref, ...), custom_call_target="tpu_custom_call" | custom-call | tf_op jit(solution)/shard_map/pallas_call | solution.py:341
  44.7 0.0 collective-permute-start.11
  44.7 1.5 collective-permute-done.11.other_ref
  46.3 0.7 copy-done.19
  46.9 1.6 shard_map.56
  48.6 1.3 collective-permute-start.12
  49.9 1.3 collective-permute-start.13
  51.2 4.1 %collective-permute-start.31 = (bf16[5,4,4,32,128]{4,3,2,1,0:T(8,128)(2,1)S(1)}, bf16[5,4,4,32,128]{4,3,2,1,0:T(8,128)(2,1)S(1)}, u32[]{:S(2)}, u32[]{:S(2)}) collective-permute-start(bf16[5,4,4,32,128]{4,3,2,1,0:T(8,128)(2,1)S(1)} %get-tuple-element.262.refs_0_.own_ref), channel_id=1, source_target_pairs={{0,2},{1,3},{2,4},{3,5},{4,6},{5,7},{6,8},{7,9},{8,10},{9,11},{10,... | collective-permute-start | bytes 1966088 | tf_op jit(solution)/shard_map/ppermute | solution.py:358
  55.3 1.3 collective-permute-start.32
  56.6 4.1 %collective-permute-start.29 = (bf16[5,4,4,32,128]{4,3,2,1,0:T(8,128)(2,1)S(1)}, bf16[5,4,4,32,128]{4,3,2,1,0:T(8,128)(2,1)S(1)}, u32[]{:S(2)}, u32[]{:S(2)}) collective-permute-start(bf16[5,4,4,32,128]{4,3,2,1,0:T(8,128)(2,1)S(1)} %get-tuple-element.263.refs_1_.own_ref), channel_id=1, source_target_pairs={{0,2},{1,3},{2,4},{3,5},{4,6},{5,7},{6,8},{7,9},{8,10},{9,11},{10,... | collective-permute-start | bytes 1966088 | tf_op jit(solution)/shard_map/ppermute | solution.py:358
  60.7 0.0 collective-permute-done.12.refs_1_
  60.7 0.0 copy-start.23
  60.7 1.3 collective-permute-start.30
  62.0 0.0 collective-permute-done.13.refs_2_
  62.0 0.6 copy-done.24
  62.6 1.6 shard_map.57.refs_0_
  64.2 13.0 %collective-permute-start.14 = (bf16[5,16,128]{2,1,0:T(8,128)(2,1)}, bf16[5,16,128]{2,1,0:T(8,128)(2,1)S(1)}, u32[]{:S(2)}, u32[]{:S(2)}) collective-permute-start(bf16[5,16,128]{2,1,0:T(8,128)(2,1)} %shard_map.57.refs_0_), channel_id=1, source_target_pairs={{16,0},{17,1},{18,2},{19,3},{20,4},{21,5},{22,6},{23,7},{24,8},{25... | collective-permute-start | bytes 61448 | tf_op jit(solution)/shard_map/ppermute | solution.py:358
  77.2 8.7 %collective-permute-done.14.refs_1_ = bf16[5,16,128]{2,1,0:T(8,128)(2,1)S(1)} collective-permute-done((bf16[5,16,128]{2,1,0:T(8,128)(2,1)}, bf16[5,16,128]{2,1,0:T(8,128)(2,1)S(1)}, u32[]{:S(2)}, u32[]{:S(2)}) %collective-permute-start.14) | collective-permute-done | bytes 20512 | tf_op jit(solution)/shard_map/ppermute | solution.py:358
  85.9 21.5 %collective-permute-start.15 = (bf16[5,16,128]{2,1,0:T(8,128)(2,1)}, bf16[5,16,128]{2,1,0:T(8,128)(2,1)S(1)}, u32[]{:S(2)}, u32[]{:S(2)}) collective-permute-start(bf16[5,16,128]{2,1,0:T(8,128)(2,1)} %shard_map.57.refs_0_), channel_id=1, source_target_pairs={{32,0},{33,1},{34,2},{35,3},{36,4},{37,5},{38,6},{39,7},{40,8},{41... | collective-permute-start | bytes 61448 | tf_op jit(solution)/shard_map/ppermute | solution.py:358
  107.4 1.5 collective-permute-done.15.refs_2_
  108.8 14.5 %collective-permute-start.16 = (bf16[5,16,128]{2,1,0:T(8,128)(2,1)}, bf16[5,16,128]{2,1,0:T(8,128)(2,1)S(1)}, u32[]{:S(2)}, u32[]{:S(2)}) collective-permute-start(bf16[5,16,128]{2,1,0:T(8,128)(2,1)} %shard_map.57.refs_0_), channel_id=1, source_target_pairs={{48,0},{49,1},{50,2},{51,3},{52,4},{53,5},{54,6},{55,7},{56,8},{57... | collective-permute-start | bytes 61448 | tf_op jit(solution)/shard_map/ppermute | solution.py:358
  123.3 1.1 collective-permute-done.16.refs_3_
  124.5 0.6 copy-done.27
  125.1 1.4 shard_map.58.refs_0_
  126.5 2.8 %collective-permute-start.17 = (bf16[4,5,16,128]{3,2,1,0:T(8,128)(2,1)}, bf16[4,5,16,128]{3,2,1,0:T(8,128)(2,1)S(1)}, u32[]{:S(2)}, u32[]{:S(2)}) collective-permute-start(bf16[4,5,16,128]{3,2,1,0:T(8,128)(2,1)} %shard_map.58.refs_0_), channel_id=1, source_target_pairs={{2,0},{3,1},{4,2},{5,3},{6,4},{7,5},{8,6},{9,7},{10,8},{11,9},{12,... | collective-permute-start | bytes 245768 | tf_op jit(solution)/shard_map/ppermute | solution.py:358
  129.2 1.8 collective-permute-done.17.refs_1_
  131.0 1.4 collective-permute-start.18
  132.5 3.0 %collective-permute-done.18.refs_2_ = bf16[4,5,16,128]{3,2,1,0:T(8,128)(2,1)S(1)} collective-permute-done((bf16[4,5,16,128]{3,2,1,0:T(8,128)(2,1)}, bf16[4,5,16,128]{3,2,1,0:T(8,128)(2,1)S(1)}, u32[]{:S(2)}, u32[]{:S(2)}) %collective-permute-start.18) | collective-permute-done | bytes 81952 | tf_op jit(solution)/shard_map/ppermute | solution.py:358
  135.5 4.0 %collective-permute-start.19 = (bf16[4,5,16,128]{3,2,1,0:T(8,128)(2,1)}, bf16[4,5,16,128]{3,2,1,0:T(8,128)(2,1)S(1)}, u32[]{:S(2)}, u32[]{:S(2)}) collective-permute-start(bf16[4,5,16,128]{3,2,1,0:T(8,128)(2,1)} %shard_map.58.refs_0_), channel_id=1, source_target_pairs={{6,0},{7,1},{8,2},{9,3},{10,4},{11,5},{12,6},{13,7},{14,8},{15,9},... | collective-permute-start | bytes 245768 | tf_op jit(solution)/shard_map/ppermute | solution.py:358
  139.5 2.9 %collective-permute-done.19.refs_3_ = bf16[4,5,16,128]{3,2,1,0:T(8,128)(2,1)S(1)} collective-permute-done((bf16[4,5,16,128]{3,2,1,0:T(8,128)(2,1)}, bf16[4,5,16,128]{3,2,1,0:T(8,128)(2,1)S(1)}, u32[]{:S(2)}, u32[]{:S(2)}) %collective-permute-start.19) | collective-permute-done | bytes 81952 | tf_op jit(solution)/shard_map/ppermute | solution.py:358
  142.4 7.1 %collective-permute-start.20 = (bf16[4,5,16,128]{3,2,1,0:T(8,128)(2,1)}, bf16[4,5,16,128]{3,2,1,0:T(8,128)(2,1)}, u32[]{:S(2)}, u32[]{:S(2)}) collective-permute-start(bf16[4,5,16,128]{3,2,1,0:T(8,128)(2,1)} %shard_map.58.refs_0_), channel_id=1, source_target_pairs={{8,0},{9,1},{10,2},{11,3},{12,4},{13,5},{14,6},{15,7},{16,8},{17,9... | collective-permute-start | bytes 245768 | tf_op jit(solution)/shard_map/ppermute | solution.py:358
  149.5 6.8 %collective-permute-done.20.refs_4_ = bf16[4,5,16,128]{3,2,1,0:T(8,128)(2,1)} collective-permute-done((bf16[4,5,16,128]{3,2,1,0:T(8,128)(2,1)}, bf16[4,5,16,128]{3,2,1,0:T(8,128)(2,1)}, u32[]{:S(2)}, u32[]{:S(2)}) %collective-permute-start.20) | collective-permute-done | bytes 81952 | tf_op jit(solution)/shard_map/ppermute | solution.py:358
  156.3 4.6 %collective-permute-start.21 = (bf16[4,5,16,128]{3,2,1,0:T(8,128)(2,1)}, bf16[4,5,16,128]{3,2,1,0:T(8,128)(2,1)}, u32[]{:S(2)}, u32[]{:S(2)}) collective-permute-start(bf16[4,5,16,128]{3,2,1,0:T(8,128)(2,1)} %shard_map.58.refs_0_), channel_id=1, source_target_pairs={{58,0},{59,1},{60,2},{61,3},{62,4},{63,5},{0,6},{1,7},{2,8},{3,9},... | collective-permute-start | bytes 245768 | tf_op jit(solution)/shard_map/ppermute | solution.py:358
  160.9 2.0 collective-permute-done.21.refs_5_
  162.9 5.7 %collective-permute-done.22.refs_6_ = bf16[4,5,16,128]{3,2,1,0:T(8,128)(2,1)} collective-permute-done((bf16[4,5,16,128]{3,2,1,0:T(8,128)(2,1)}, bf16[4,5,16,128]{3,2,1,0:T(8,128)(2,1)}, u32[]{:S(2)}, u32[]{:S(2)}) %collective-permute-start.22) | collective-permute-done | bytes 81952 | tf_op jit(solution)/shard_map/ppermute | solution.py:358
  168.6 0.0 collective-permute-start.23
  168.7 6.5 %collective-permute-done.23.refs_7_ = bf16[4,5,16,128]{3,2,1,0:T(8,128)(2,1)} collective-permute-done((bf16[4,5,16,128]{3,2,1,0:T(8,128)(2,1)}, bf16[4,5,16,128]{3,2,1,0:T(8,128)(2,1)}, u32[]{:S(2)}, u32[]{:S(2)}) %collective-permute-start.23) | collective-permute-done | bytes 81952 | tf_op jit(solution)/shard_map/ppermute | solution.py:358
  175.2 2.1 shard_map.59.own_ref
  177.2 2.2 collective-permute-start.27
  179.5 0.0 collective-permute-done.31.before_ref
  179.5 1.3 collective-permute-start.28
  180.8 0.0 collective-permute-done.32.after_ref
  180.8 4.9 %collective-permute-start.25 = (bf16[5,4,4,32,128]{4,3,2,1,0:T(8,128)(2,1)S(1)}, bf16[5,4,4,32,128]{4,3,2,1,0:T(8,128)(2,1)}, u32[]{:S(2)}, u32[]{:S(2)}) collective-permute-start(bf16[5,4,4,32,128]{4,3,2,1,0:T(8,128)(2,1)S(1)} %get-tuple-element.265.refs_3_.own_ref), channel_id=1, source_target_pairs={{0,2},{1,3},{2,4},{3,5},{4,6},{5,7},{6,8},{7,9},{8,10},{9,11},{10,... | collective-permute-start | bytes 1966088 | tf_op jit(solution)/shard_map/ppermute | solution.py:358
  185.7 1.3 collective-permute-start.26
  187.0 0.8 copy-done.13
  187.9 16.8 %collective-permute-start.24 = (bf16[32,5,16,128]{3,2,1,0:T(8,128)(2,1)}, bf16[32,5,16,128]{3,2,1,0:T(8,128)(2,1)}, u32[]{:S(2)}, u32[]{:S(2)}) collective-permute-start(bf16[32,5,16,128]{3,2,1,0:T(8,128)(2,1)} %shard_map.59.own_ref), channel_id=1, source_target_pairs={{1,0},{0,1},{3,2},{2,3},{5,4},{4,5},{7,6},{6,7},{9,8},{8,9},{11,10... | collective-permute-start | bytes 1966088 | tf_op jit(solution)/shard_map/ppermute | solution.py:358
  204.7 4.1 %scores.4.refs_0_ = bf16[4,32,32,384]{3,2,1,0:T(8,128)(2,1)} custom-call(s32[2,128]{1,0:T(2,128)} %reshape.8.bounds_ref, bf16[5,4,4,32,128]{4,3,2,1,0:T(8,128)(2,1)S(1)} %get-tuple-element.262.refs_0_.own_ref, bf16[5,4,4,32,128]{4,3,2,1,0:T(8,128)(2,1)} %copy-done.14, bf16[5,4,4,32,128]{4,3,2,1,0:T(8,128)(2,1)} %copy-done.15), custom_call_target="tpu_custom_call" | custom-call | tf_op jit(solution)/shard_map/scores/pallas_call | solution.py:304
  208.8 4.1 %scores.5.refs_0_ = bf16[4,32,32,384]{3,2,1,0:T(8,128)(2,1)} custom-call(s32[2,128]{1,0:T(2,128)} %reshape.8.bounds_ref, bf16[5,4,4,32,128]{4,3,2,1,0:T(8,128)(2,1)S(1)} %get-tuple-element.263.refs_1_.own_ref, bf16[5,4,4,32,128]{4,3,2,1,0:T(8,128)(2,1)} %copy-done.12, bf16[5,4,4,32,128]{4,3,2,1,0:T(8,128)(2,1)} %copy-done.13, ...), custom_call_target="tpu_custom_call", output_to_operand_aliasing={{}: (4, {})} | custom-call | tf_op jit(solution)/shard_map/scores/pallas_call | solution.py:304
  212.9 0.0 collective-permute-done.27.before_ref
  212.9 4.1 %scores.6.refs_0_ = bf16[4,32,32,384]{3,2,1,0:T(8,128)(2,1)} custom-call(s32[2,128]{1,0:T(2,128)} %reshape.8.bounds_ref, bf16[5,4,4,32,128]{4,3,2,1,0:T(8,128)(2,1)S(1)} %get-tuple-element.264.refs_2_.own_ref, bf16[5,4,4,32,128]{4,3,2,1,0:T(8,128)(2,1)} %collective-permute-done.27.before_ref, ...), custom_call_target="tpu_custom_call", output_to_operand_aliasing={{}: (4, {})} | custom-call | tf_op jit(solution)/shard_map/scores/pallas_call | solution.py:304
  217.1 0.0 collective-permute-done.25.before_ref
  217.1 0.0 collective-permute-done.26.after_ref
  217.1 4.1 %scores.7.score_ref = bf16[4,32,32,384]{3,2,1,0:T(8,128)(2,1)} custom-call(s32[2,128]{1,0:T(2,128)} %reshape.8.bounds_ref, bf16[5,4,4,32,128]{4,3,2,1,0:T(8,128)(2,1)S(1)} %get-tuple-element.265.refs_3_.own_ref, bf16[5,4,4,32,128]{4,3,2,1,0:T(8,128)(2,1)} %collective-permute-done.25.before_ref, ...), custom_call_target="tpu_custom_call", output_to_operand_aliasing={{}: (4, {})} | custom-call | tf_op jit(solution)/shard_map/scores/pallas_call | solution.py:304
  221.2 4.3 %order.2 = bf16[384,1024]{1,0:T(8,128)(2,1)S(1)} custom-call(s32[3]{0:T(128)} %pad_add_fusion.1.place_ref, s32[1,1024]{1,0:T(1,128)S(1)} %bitcast.22, s32[32,1024]{1,0:T(8,128)S(1)} %get-tuple-element.261.rank_ref, bf16[32,5,16,128]{3,2,1,0:T(8,128)(2,1)} %shard_map.59.own_ref, bf16[32,5,16,128]{3,2,1,0:T(8,128)(2,1)} %collective-permute-done.24.other_ref), custom_call_target="tpu_custom_call" | custom-call | tf_op jit(solution)/shard_map/order/pallas_call | solution.py:250
  225.5 0.8 while.10
  226.4 9.8 %correlate.1 = bf16[4,32,32,1024]{3,2,1,0:T(8,128)(2,1)} custom-call(bf16[384,1024]{1,0:T(8,128)(2,1)S(1)} %get-tuple-element.121.table_ref, bf16[4,32,32,384]{3,2,1,0:T(8,128)(2,1)} %scores.7.score_ref), custom_call_target="tpu_custom_call" | custom-call | tf_op jit(solution)/shard_map/correlate/pallas_call | solution.py:324
  (38 shorter events, 0.1 us)
Async XLA Ops:
  1.2 25.5 %collective-permute-start.10 = (f32[4,4,32,300]{3,2,1,0:T(8,128)S(1)}, f32[4,4,32,300]{3,2,1,0:T(8,128)S(1)}, u32[]{:S(2)}, u32[]{:S(2)}) collective-permute-start(f32[4,4,32,300]{3,2,1,0:T(8,128)S(1)} %dynamic-slice_bitcast_fusion), channel_id=1, source_target_pairs={{1,0},{0,1},{3,2},{2,3},{5,4},{4,5},{7,6},{6,7},{9,8},{8,9},{11,10... | collective-permute-start | bytes 1843208 | tf_op jit(solution)/shard_map/ppermute | solution.py:358
  26.7 0.9 copy-start.11
  27.6 12.4 %copy-start.10 = (s32[1024]{0:T(1024)S(1)}, s32[1024]{0:T(1024)}, u32[]{:S(2)}) copy-start(s32[1024]{0:T(1024)} %param.9) | copy-start | bytes 12292
  40.0 137.2 %copy-start = (bf16[5,4,4,32,128]{4,3,2,1,0:T(8,128)(2,1)}, bf16[5,4,4,32,128]{4,3,2,1,0:T(8,128)(2,1)S(1)}, u32[]{:S(2)}) copy-start(bf16[5,4,4,32,128]{4,3,2,1,0:T(8,128)(2,1)S(1)} %get-tuple-element.266.refs_4_) | copy-start | bytes 1966084
  40.0 137.2 %copy-start.1 = (bf16[5,4,4,32,128]{4,3,2,1,0:T(8,128)(2,1)}, bf16[5,4,4,32,128]{4,3,2,1,0:T(8,128)(2,1)S(1)}, u32[]{:S(2)}) copy-start(bf16[5,4,4,32,128]{4,3,2,1,0:T(8,128)(2,1)S(1)} %get-tuple-element.267.refs_5_) | copy-start | bytes 1966084
  40.0 137.2 %copy-start.2 = (bf16[5,4,4,32,128]{4,3,2,1,0:T(8,128)(2,1)}, bf16[5,4,4,32,128]{4,3,2,1,0:T(8,128)(2,1)S(1)}, u32[]{:S(2)}) copy-start(bf16[5,4,4,32,128]{4,3,2,1,0:T(8,128)(2,1)S(1)} %get-tuple-element.268.refs_6_) | copy-start | bytes 1966084
  40.0 137.2 %copy-start.3 = (bf16[5,4,4,32,128]{4,3,2,1,0:T(8,128)(2,1)}, bf16[5,4,4,32,128]{4,3,2,1,0:T(8,128)(2,1)S(1)}, u32[]{:S(2)}) copy-start(bf16[5,4,4,32,128]{4,3,2,1,0:T(8,128)(2,1)S(1)} %get-tuple-element.269.refs_7_) | copy-start | bytes 1966084
  44.7 1.6 collective-permute-start.11
  46.3 0.7 copy-start.19
  48.6 12.1 %collective-permute-start.12 = (f32[32,384]{1,0:T(8,128)}, f32[32,384]{1,0:T(8,128)S(1)}, u32[]{:S(2)}, u32[]{:S(2)}) collective-permute-start(f32[32,384]{1,0:T(8,128)} %get-tuple-element.118), channel_id=1, source_target_pairs={{0,2},{1,3},{2,4},{3,5},{4,6},{5,7},{6,8},{7,9},{8,10},{9,11},{10,... | collective-permute-start | bytes 147464 | tf_op jit(solution)/shard_map/ppermute | solution.py:358
  49.9 12.1 %collective-permute-start.13 = (f32[32,384]{1,0:T(8,128)}, f32[32,384]{1,0:T(8,128)S(1)}, u32[]{:S(2)}, u32[]{:S(2)}) collective-permute-start(f32[32,384]{1,0:T(8,128)} %get-tuple-element.119), channel_id=1, source_target_pairs={{2,0},{3,1},{4,2},{5,3},{6,4},{7,5},{8,6},{9,7},{10,8},{11,9},{12,... | collective-permute-start | bytes 147464 | tf_op jit(solution)/shard_map/ppermute | solution.py:358
  51.2 128.3 %collective-permute-start.31 = (bf16[5,4,4,32,128]{4,3,2,1,0:T(8,128)(2,1)S(1)}, bf16[5,4,4,32,128]{4,3,2,1,0:T(8,128)(2,1)S(1)}, u32[]{:S(2)}, u32[]{:S(2)}) collective-permute-start(bf16[5,4,4,32,128]{4,3,2,1,0:T(8,128)(2,1)S(1)} %get-tuple-element.262.refs_0_.own_ref), channel_id=1, source_target_pairs={{0,2},{1,3},{2,4},{3,5},{4,6},{5,7},{6,8},{7,9},{8,10},{9,11},{10,... | collective-permute-start | bytes 1966088 | tf_op jit(solution)/shard_map/ppermute | solution.py:358
  55.3 125.5 %collective-permute-start.32 = (bf16[5,4,4,32,128]{4,3,2,1,0:T(8,128)(2,1)S(1)}, bf16[5,4,4,32,128]{4,3,2,1,0:T(8,128)(2,1)S(1)}, u32[]{:S(2)}, u32[]{:S(2)}) collective-permute-start(bf16[5,4,4,32,128]{4,3,2,1,0:T(8,128)(2,1)S(1)} %get-tuple-element.262.refs_0_.own_ref), channel_id=1, source_target_pairs={{2,0},{3,1},{4,2},{5,3},{6,4},{7,5},{8,6},{9,7},{10,8},{11,9},{12,... | collective-permute-start | bytes 1966088 | tf_op jit(solution)/shard_map/ppermute | solution.py:358
  56.6 129.1 %collective-permute-start.29 = (bf16[5,4,4,32,128]{4,3,2,1,0:T(8,128)(2,1)S(1)}, bf16[5,4,4,32,128]{4,3,2,1,0:T(8,128)(2,1)S(1)}, u32[]{:S(2)}, u32[]{:S(2)}) collective-permute-start(bf16[5,4,4,32,128]{4,3,2,1,0:T(8,128)(2,1)S(1)} %get-tuple-element.263.refs_1_.own_ref), channel_id=1, source_target_pairs={{0,2},{1,3},{2,4},{3,5},{4,6},{5,7},{6,8},{7,9},{8,10},{9,11},{10,... | collective-permute-start | bytes 1966088 | tf_op jit(solution)/shard_map/ppermute | solution.py:358
  60.7 1.4 copy-start.23
  60.7 126.3 %collective-permute-start.30 = (bf16[5,4,4,32,128]{4,3,2,1,0:T(8,128)(2,1)S(1)}, bf16[5,4,4,32,128]{4,3,2,1,0:T(8,128)(2,1)S(1)}, u32[]{:S(2)}, u32[]{:S(2)}) collective-permute-start(bf16[5,4,4,32,128]{4,3,2,1,0:T(8,128)(2,1)S(1)} %get-tuple-element.263.refs_1_.own_ref), channel_id=1, source_target_pairs={{2,0},{3,1},{4,2},{5,3},{6,4},{7,5},{8,6},{9,7},{10,8},{11,9},{12,... | collective-permute-start | bytes 1966088 | tf_op jit(solution)/shard_map/ppermute | solution.py:358
  62.0 0.6 copy-start.24
  64.2 21.6 %collective-permute-start.14 = (bf16[5,16,128]{2,1,0:T(8,128)(2,1)}, bf16[5,16,128]{2,1,0:T(8,128)(2,1)S(1)}, u32[]{:S(2)}, u32[]{:S(2)}) collective-permute-start(bf16[5,16,128]{2,1,0:T(8,128)(2,1)} %shard_map.57.refs_0_), channel_id=1, source_target_pairs={{16,0},{17,1},{18,2},{19,3},{20,4},{21,5},{22,6},{23,7},{24,8},{25... | collective-permute-start | bytes 61448 | tf_op jit(solution)/shard_map/ppermute | solution.py:358
  85.9 38.6 %copy-start.25 = (bf16[5,16,128]{2,1,0:T(8,128)(2,1)}, bf16[5,16,128]{2,1,0:T(8,128)(2,1)S(1)}, u32[]{:S(2)}) copy-start(bf16[5,16,128]{2,1,0:T(8,128)(2,1)S(1)} %collective-permute-done.14.refs_1_) | copy-start | bytes 61444
  85.9 23.0 %collective-permute-start.15 = (bf16[5,16,128]{2,1,0:T(8,128)(2,1)}, bf16[5,16,128]{2,1,0:T(8,128)(2,1)S(1)}, u32[]{:S(2)}, u32[]{:S(2)}) collective-permute-start(bf16[5,16,128]{2,1,0:T(8,128)(2,1)} %shard_map.57.refs_0_), channel_id=1, source_target_pairs={{32,0},{33,1},{34,2},{35,3},{36,4},{37,5},{38,6},{39,7},{40,8},{41... | collective-permute-start | bytes 61448 | tf_op jit(solution)/shard_map/ppermute | solution.py:358
  108.8 15.6 %copy-start.26 = (bf16[5,16,128]{2,1,0:T(8,128)(2,1)}, bf16[5,16,128]{2,1,0:T(8,128)(2,1)S(1)}, u32[]{:S(2)}) copy-start(bf16[5,16,128]{2,1,0:T(8,128)(2,1)S(1)} %collective-permute-done.15.refs_2_) | copy-start | bytes 61444
  108.8 15.6 %collective-permute-start.16 = (bf16[5,16,128]{2,1,0:T(8,128)(2,1)}, bf16[5,16,128]{2,1,0:T(8,128)(2,1)S(1)}, u32[]{:S(2)}, u32[]{:S(2)}) collective-permute-start(bf16[5,16,128]{2,1,0:T(8,128)(2,1)} %shard_map.57.refs_0_), channel_id=1, source_target_pairs={{48,0},{49,1},{50,2},{51,3},{52,4},{53,5},{54,6},{55,7},{56,8},{57... | collective-permute-start | bytes 61448 | tf_op jit(solution)/shard_map/ppermute | solution.py:358
  124.5 0.6 copy-start.27
  126.5 4.6 %collective-permute-start.17 = (bf16[4,5,16,128]{3,2,1,0:T(8,128)(2,1)}, bf16[4,5,16,128]{3,2,1,0:T(8,128)(2,1)S(1)}, u32[]{:S(2)}, u32[]{:S(2)}) collective-permute-start(bf16[4,5,16,128]{3,2,1,0:T(8,128)(2,1)} %shard_map.58.refs_0_), channel_id=1, source_target_pairs={{2,0},{3,1},{4,2},{5,3},{6,4},{7,5},{8,6},{9,7},{10,8},{11,9},{12,... | collective-permute-start | bytes 245768 | tf_op jit(solution)/shard_map/ppermute | solution.py:358
  131.0 44.1 %copy-start.20 = (bf16[4,5,16,128]{3,2,1,0:T(8,128)(2,1)}, bf16[4,5,16,128]{3,2,1,0:T(8,128)(2,1)S(1)}, u32[]{:S(2)}) copy-start(bf16[4,5,16,128]{3,2,1,0:T(8,128)(2,1)S(1)} %collective-permute-done.17.refs_1_) | copy-start | bytes 245764
  131.0 4.4 %collective-permute-start.18 = (bf16[4,5,16,128]{3,2,1,0:T(8,128)(2,1)}, bf16[4,5,16,128]{3,2,1,0:T(8,128)(2,1)S(1)}, u32[]{:S(2)}, u32[]{:S(2)}) collective-permute-start(bf16[4,5,16,128]{3,2,1,0:T(8,128)(2,1)} %shard_map.58.refs_0_), channel_id=1, source_target_pairs={{4,0},{5,1},{6,2},{7,3},{8,4},{9,5},{10,6},{11,7},{12,8},{13,9},{1... | collective-permute-start | bytes 245768 | tf_op jit(solution)/shard_map/ppermute | solution.py:358
  135.5 39.7 %copy-start.21 = (bf16[4,5,16,128]{3,2,1,0:T(8,128)(2,1)}, bf16[4,5,16,128]{3,2,1,0:T(8,128)(2,1)S(1)}, u32[]{:S(2)}) copy-start(bf16[4,5,16,128]{3,2,1,0:T(8,128)(2,1)S(1)} %collective-permute-done.18.refs_2_) | copy-start | bytes 245764
  135.5 6.9 %collective-permute-start.19 = (bf16[4,5,16,128]{3,2,1,0:T(8,128)(2,1)}, bf16[4,5,16,128]{3,2,1,0:T(8,128)(2,1)S(1)}, u32[]{:S(2)}, u32[]{:S(2)}) collective-permute-start(bf16[4,5,16,128]{3,2,1,0:T(8,128)(2,1)} %shard_map.58.refs_0_), channel_id=1, source_target_pairs={{6,0},{7,1},{8,2},{9,3},{10,4},{11,5},{12,6},{13,7},{14,8},{15,9},... | collective-permute-start | bytes 245768 | tf_op jit(solution)/shard_map/ppermute | solution.py:358
  142.4 32.8 %copy-start.22 = (bf16[4,5,16,128]{3,2,1,0:T(8,128)(2,1)}, bf16[4,5,16,128]{3,2,1,0:T(8,128)(2,1)S(1)}, u32[]{:S(2)}) copy-start(bf16[4,5,16,128]{3,2,1,0:T(8,128)(2,1)S(1)} %collective-permute-done.19.refs_3_) | copy-start | bytes 245764
  142.4 13.9 %collective-permute-start.20 = (bf16[4,5,16,128]{3,2,1,0:T(8,128)(2,1)}, bf16[4,5,16,128]{3,2,1,0:T(8,128)(2,1)}, u32[]{:S(2)}, u32[]{:S(2)}) collective-permute-start(bf16[4,5,16,128]{3,2,1,0:T(8,128)(2,1)} %shard_map.58.refs_0_), channel_id=1, source_target_pairs={{8,0},{9,1},{10,2},{11,3},{12,4},{13,5},{14,6},{15,7},{16,8},{17,9... | collective-permute-start | bytes 245768 | tf_op jit(solution)/shard_map/ppermute | solution.py:358
  156.3 6.6 %collective-permute-start.21 = (bf16[4,5,16,128]{3,2,1,0:T(8,128)(2,1)}, bf16[4,5,16,128]{3,2,1,0:T(8,128)(2,1)}, u32[]{:S(2)}, u32[]{:S(2)}) collective-permute-start(bf16[4,5,16,128]{3,2,1,0:T(8,128)(2,1)} %shard_map.58.refs_0_), channel_id=1, source_target_pairs={{58,0},{59,1},{60,2},{61,3},{62,4},{63,5},{0,6},{1,7},{2,8},{3,9},... | collective-permute-start | bytes 245768 | tf_op jit(solution)/shard_map/ppermute | solution.py:358
  162.9 5.7 %collective-permute-start.22 = (bf16[4,5,16,128]{3,2,1,0:T(8,128)(2,1)}, bf16[4,5,16,128]{3,2,1,0:T(8,128)(2,1)}, u32[]{:S(2)}, u32[]{:S(2)}) collective-permute-start(bf16[4,5,16,128]{3,2,1,0:T(8,128)(2,1)} %shard_map.58.refs_0_), channel_id=1, source_target_pairs={{60,0},{61,1},{62,2},{63,3},{0,4},{1,5},{2,6},{3,7},{4,8},{5,9},{6... | collective-permute-start | bytes 245768 | tf_op jit(solution)/shard_map/ppermute | solution.py:358
  168.6 6.5 %collective-permute-start.23 = (bf16[4,5,16,128]{3,2,1,0:T(8,128)(2,1)}, bf16[4,5,16,128]{3,2,1,0:T(8,128)(2,1)}, u32[]{:S(2)}, u32[]{:S(2)}) collective-permute-start(bf16[4,5,16,128]{3,2,1,0:T(8,128)(2,1)} %shard_map.58.refs_0_), channel_id=1, source_target_pairs={{62,0},{63,1},{0,2},{1,3},{2,4},{3,5},{4,6},{5,7},{6,8},{7,9},{8,1... | collective-permute-start | bytes 245768 | tf_op jit(solution)/shard_map/ppermute | solution.py:358
  177.2 35.7 %collective-permute-start.27 = (bf16[5,4,4,32,128]{4,3,2,1,0:T(8,128)(2,1)S(1)}, bf16[5,4,4,32,128]{4,3,2,1,0:T(8,128)(2,1)}, u32[]{:S(2)}, u32[]{:S(2)}) collective-permute-start(bf16[5,4,4,32,128]{4,3,2,1,0:T(8,128)(2,1)S(1)} %get-tuple-element.264.refs_2_.own_ref), channel_id=1, source_target_pairs={{0,2},{1,3},{2,4},{3,5},{4,6},{5,7},{6,8},{7,9},{8,10},{9,11},{10,... | collective-permute-start | bytes 1966088 | tf_op jit(solution)/shard_map/ppermute | solution.py:358
  179.5 7.5 %copy-start.14 = (bf16[5,4,4,32,128]{4,3,2,1,0:T(8,128)(2,1)}, bf16[5,4,4,32,128]{4,3,2,1,0:T(8,128)(2,1)S(1)}, u32[]{:S(2)}) copy-start(bf16[5,4,4,32,128]{4,3,2,1,0:T(8,128)(2,1)S(1)} %collective-permute-done.31.before_ref) | copy-start | bytes 1966084
  179.5 33.5 %collective-permute-start.28 = (bf16[5,4,4,32,128]{4,3,2,1,0:T(8,128)(2,1)S(1)}, bf16[5,4,4,32,128]{4,3,2,1,0:T(8,128)(2,1)}, u32[]{:S(2)}, u32[]{:S(2)}) collective-permute-start(bf16[5,4,4,32,128]{4,3,2,1,0:T(8,128)(2,1)S(1)} %get-tuple-element.264.refs_2_.own_ref), channel_id=1, source_target_pairs={{2,0},{3,1},{4,2},{5,3},{6,4},{7,5},{8,6},{9,7},{10,8},{11,9},{12,... | collective-permute-start | bytes 1966088 | tf_op jit(solution)/shard_map/ppermute | solution.py:358
  180.8 6.2 %copy-start.15 = (bf16[5,4,4,32,128]{4,3,2,1,0:T(8,128)(2,1)}, bf16[5,4,4,32,128]{4,3,2,1,0:T(8,128)(2,1)S(1)}, u32[]{:S(2)}) copy-start(bf16[5,4,4,32,128]{4,3,2,1,0:T(8,128)(2,1)S(1)} %collective-permute-done.32.after_ref) | copy-start | bytes 1966084
  180.8 36.3 %collective-permute-start.25 = (bf16[5,4,4,32,128]{4,3,2,1,0:T(8,128)(2,1)S(1)}, bf16[5,4,4,32,128]{4,3,2,1,0:T(8,128)(2,1)}, u32[]{:S(2)}, u32[]{:S(2)}) collective-permute-start(bf16[5,4,4,32,128]{4,3,2,1,0:T(8,128)(2,1)S(1)} %get-tuple-element.265.refs_3_.own_ref), channel_id=1, source_target_pairs={{0,2},{1,3},{2,4},{3,5},{4,6},{5,7},{6,8},{7,9},{8,10},{9,11},{10,... | collective-permute-start | bytes 1966088 | tf_op jit(solution)/shard_map/ppermute | solution.py:358
  185.7 23.1 %copy-start.12 = (bf16[5,4,4,32,128]{4,3,2,1,0:T(8,128)(2,1)}, bf16[5,4,4,32,128]{4,3,2,1,0:T(8,128)(2,1)S(1)}, u32[]{:S(2)}) copy-start(bf16[5,4,4,32,128]{4,3,2,1,0:T(8,128)(2,1)S(1)} %collective-permute-done.29.before_ref) | copy-start | bytes 1966084
  185.7 31.4 %collective-permute-start.26 = (bf16[5,4,4,32,128]{4,3,2,1,0:T(8,128)(2,1)S(1)}, bf16[5,4,4,32,128]{4,3,2,1,0:T(8,128)(2,1)}, u32[]{:S(2)}, u32[]{:S(2)}) collective-permute-start(bf16[5,4,4,32,128]{4,3,2,1,0:T(8,128)(2,1)S(1)} %get-tuple-element.265.refs_3_.own_ref), channel_id=1, source_target_pairs={{2,0},{3,1},{4,2},{5,3},{6,4},{7,5},{8,6},{9,7},{10,8},{11,9},{12,... | collective-permute-start | bytes 1966088 | tf_op jit(solution)/shard_map/ppermute | solution.py:358
  187.0 0.8 copy-start.13
  187.9 33.3 %collective-permute-start.24 = (bf16[32,5,16,128]{3,2,1,0:T(8,128)(2,1)}, bf16[32,5,16,128]{3,2,1,0:T(8,128)(2,1)}, u32[]{:S(2)}, u32[]{:S(2)}) collective-permute-start(bf16[32,5,16,128]{3,2,1,0:T(8,128)(2,1)} %shard_map.59.own_ref), channel_id=1, source_target_pairs={{1,0},{0,1},{3,2},{2,3},{5,4},{4,5},{7,6},{6,7},{9,8},{8,9},{11,10... | collective-permute-start | bytes 1966088 | tf_op jit(solution)/shard_map/ppermute | solution.py:358
